TPU v7x, 32 devices: a whole 2x2x4 slice. The times are simulated.
32 devices in a mesh: dp: 32 (over z, y, x, core).
Axes of the slice: x: 2, y: 2, z: 4, core: 2. Of those that a mesh axis runs over, the one named last changes fastest.
Arguments:
- tokens: bfloat16 [8192, 1024], P('dp'), may hold values from -6 to 6
- cotangent: bfloat16 [8192, 1024], P('dp'), may hold values from -6 to 6
- lengths: int32 [64], P('dp'), may hold values from 64 to 128, as said below
- vectors: float32 [8, 1024], P(None, 'dp')
- bias_up: float32 [4096], P('dp'), may hold values from -3 to 3
- w_qkv: float32 [1024, 3072], P('dp')
- w_out: float32 [1024, 1024], P('dp'), may hold values from -0.5 to 0.5
- w_up: float32 [1024, 4096], P('dp'), may hold values from -0.1875 to 0.1875
- w_down: float32 [4096, 1024], P('dp'), may hold values from -0.09375 to 0.09375
- mom_vectors: float32 [2, 8, 1024], P(None, None, 'dp'), as said below
- mom_bias_up: float32 [2, 4096], P(None, 'dp'), as said below
- mom_qkv: float32 [2, 1024, 3072], P(None, 'dp'), as said below
- mom_out: float32 [2, 1024, 1024], P(None, 'dp'), as said below
- mom_up: float32 [2, 1024, 4096], P(None, 'dp'), as said below
- mom_down: float32 [2, 4096, 1024], P(None, 'dp'), as said below
Outputs:
- output: bfloat16 [8192, 1024], P('dp')
- input_grad: float32 [8192, 1024], P('dp')
- grad_vectors: float32 [8, 1024], P(None, 'dp')
- grad_bias_up: float32 [4096], P('dp')
- grad_qkv: float32 [1024, 3072], P('dp')
- grad_out: float32 [1024, 1024], P('dp')
- grad_up: float32 [1024, 4096], P('dp')
- grad_down: float32 [4096, 1024], P('dp')
- update_vectors: float32 [8, 1024], P(None, 'dp')
- update_bias_up: float32 [4096], P('dp')
- update_qkv: float32 [1024, 3072], P('dp')
- update_out: float32 [1024, 1024], P('dp')
- update_up: float32 [1024, 4096], P('dp')
- update_down: float32 [4096, 1024], P('dp')
- new_first_vectors: float32 [8, 1024], P(None, 'dp')
- new_first_bias_up: float32 [4096], P('dp')
- new_first_qkv: float32 [1024, 3072], P('dp')
- new_first_out: float32 [1024, 1024], P('dp')
- new_first_up: float32 [1024, 4096], P('dp')
- new_first_down: float32 [4096, 1024], P('dp')
- new_second_vectors: float32 [8, 1024], P(None, 'dp')
- new_second_bias_up: float32 [4096], P('dp')
- new_second_qkv: float32 [1024, 3072], P('dp')
- new_second_out: float32 [1024, 1024], P('dp')
- new_second_up: float32 [1024, 4096], P('dp')
- new_second_down: float32 [4096, 1024], P('dp')
Inputs may be any that keep to these rules, and one draw needn't show every extreme that they name: `lengths`: some slot has exactly 128. `mom_vectors`: every second moment is positive. `mom_bias_up`: every second moment is positive. `mom_qkv`: every second moment is positive. `mom_out`: every second moment is positive. `mom_up`: every second moment is positive. `mom_down`: every second moment is positive.
All inputs are finite; a program needn't handle non-finite values.
Results may differ from a plain program's by a relative error of at most 0.02.
The roundings to bfloat16 on the way count: a program that leaves them out, or rounds other values in their place, can miss the bound.
Values may be sent and summed in bfloat16 or wider, within the bound.
A program may use at most 192 MiB of HBM per device.

v0:
```python
import math

import jax
import jax.numpy as jnp
from jax import lax
from jax.sharding import PartitionSpec as P

D = 1024
HEADS = 16
HEAD_DIM = 64
MB_ROWS = 128
MICRO = 2
STEP = 3


ln_eps = 1e-05
gelu_c = math.sqrt(2.0 / math.pi)
beta_one = 0.9
beta_two = 0.95
decay_rate = 0.1
adam_eps = 1e-08


def product(left, right):
    return jnp.dot(left, right, preferred_element_type=jnp.float32)


def contract(form, left, right):
    return jnp.einsum(form, left, right, preferred_element_type=jnp.float32)


def layer_norm(values, gain, shift):
    centred = values - jnp.mean(values, axis=-1, keepdims=True)
    rstd = lax.rsqrt(jnp.mean(centred * centred, axis=-1, keepdims=True) + ln_eps)
    normed = centred * rstd
    return (normed * gain + shift, normed, rstd)


def norm_back(grad_in, normed, rstd, gain):
    scaled = grad_in * gain
    inner = (
        scaled
        - jnp.mean(scaled, axis=-1, keepdims=True)
        - normed * jnp.mean(scaled * normed, axis=-1, keepdims=True)
    )
    return rstd * inner


def gelu_pair(pre):
    tanh_val = jnp.tanh(gelu_c * (pre + 0.044715 * pre * pre * pre))
    value = 0.5 * pre * (1.0 + tanh_val)
    slope = 0.5 * (1.0 + tanh_val) + 0.5 * pre * (1.0 - tanh_val * tanh_val) * gelu_c * (
        1.0 + 3.0 * 0.044715 * pre * pre
    )
    return (value, slope)


def alibi_bias(rows):
    place = jnp.arange(rows)
    dist = (place[:, None] - place[None, :]).astype(jnp.float32)
    slopes = jnp.exp2(-8.0 * (jnp.arange(HEADS) + 1).astype(jnp.float32) / HEADS)
    bias = -slopes[:, None, None] * dist[None]
    return jnp.where(dist[None] >= 0, bias, -1e30)


def attention_scores(q3, k3, alibi):
    return contract("qhd,khd->hqk", q3, k3) * (1.0 / math.sqrt(HEAD_DIM)) + alibi


def forward_block(x_rows, weights, alibi):
    vec, up_bias, qkv_w, out_w, up_w, down_w = weights
    vecf = vec.astype(jnp.float32)
    rows = x_rows.shape[0]
    xf = x_rows.astype(jnp.float32)
    ln_one, normed_one, rstd_one = layer_norm(xf, vecf[0], vecf[1])
    a_one = ln_one.astype(jnp.bfloat16)
    qkv = product(a_one, qkv_w)
    query = (qkv[:, :D] + vecf[2]).astype(jnp.bfloat16).reshape(rows, HEADS, HEAD_DIM)
    keyx = qkv[:, D : 2 * D].astype(jnp.bfloat16).reshape(rows, HEADS, HEAD_DIM)
    value = (qkv[:, 2 * D :] + vecf[3]).astype(jnp.bfloat16).reshape(rows, HEADS, HEAD_DIM)
    scores = attention_scores(query, keyx, alibi)
    top = jnp.max(scores, axis=-1, keepdims=True)
    lse = top + jnp.log(jnp.sum(jnp.exp(scores - top), axis=-1, keepdims=True))
    probs = jnp.exp(scores - lse).astype(jnp.bfloat16)
    attn = contract("hqk,khd->qhd", probs, value).reshape(rows, D).astype(jnp.bfloat16)
    h_one = xf + product(attn, out_w) + vecf[4]
    ln_two, normed_two, rstd_two = layer_norm(h_one, vecf[5], vecf[6])
    a_two = ln_two.astype(jnp.bfloat16)
    pre = product(a_two, up_w) + up_bias.astype(jnp.float32)
    act, slope = gelu_pair(pre)
    act_b = act.astype(jnp.bfloat16)
    out = (h_one + product(act_b, down_w) + vecf[7]).astype(jnp.bfloat16)
    saved = (
        normed_one,
        rstd_one,
        a_one,
        query,
        keyx,
        value,
        lse,
        attn,
        normed_two,
        rstd_two,
        a_two,
        slope,
        act_b,
    )
    return (out, saved)


def backward_block(saved, grad_rows, weights, alibi):
    vec, up_bias, qkv_w, out_w, up_w, down_w = weights
    vecf = vec.astype(jnp.float32)
    (
        normed_one,
        rstd_one,
        a_one,
        query,
        keyx,
        value,
        lse,
        attn,
        normed_two,
        rstd_two,
        a_two,
        slope,
        act_b,
    ) = saved
    rows = grad_rows.shape[0]
    scale = 1.0 / math.sqrt(HEAD_DIM)
    dyf = grad_rows.astype(jnp.float32)
    g_bdown = jnp.sum(dyf, axis=0)
    g_down = product(act_b.T, grad_rows)
    d_pre = product(grad_rows, down_w.T) * slope
    g_bup = jnp.sum(d_pre, axis=0)
    d_pre_b = d_pre.astype(jnp.bfloat16)
    g_up = product(a_two.T, d_pre_b)
    d_a2 = product(d_pre_b, up_w.T)
    g_ln2g = jnp.sum(d_a2 * normed_two, axis=0)
    g_ln2b = jnp.sum(d_a2, axis=0)
    d_h1 = dyf + norm_back(d_a2, normed_two, rstd_two, vecf[5])
    g_bout = jnp.sum(d_h1, axis=0)
    d_h1_b = d_h1.astype(jnp.bfloat16)
    g_out = product(attn.T, d_h1_b)
    d_attn = product(d_h1_b, out_w.T).astype(jnp.bfloat16).reshape(rows, HEADS, HEAD_DIM)
    probs_f = jnp.exp(attention_scores(query, keyx, alibi) - lse)
    probs = probs_f.astype(jnp.bfloat16)
    d_v = contract("hqk,qhd->khd", probs, d_attn).reshape(rows, D)
    d_probs = contract("qhd,khd->hqk", d_attn, value)
    delta = jnp.sum(
        d_attn.astype(jnp.float32) * attn.reshape(rows, HEADS, HEAD_DIM).astype(jnp.float32),
        axis=-1,
    ).T[:, :, None]
    d_scores = (probs_f * (d_probs - delta)).astype(jnp.bfloat16)
    d_q = (contract("hqk,khd->qhd", d_scores, keyx) * scale).reshape(rows, D)
    d_k = (contract("hqk,qhd->khd", d_scores, query) * scale).reshape(rows, D)
    g_bq = jnp.sum(d_q, axis=0)
    g_bv = jnp.sum(d_v, axis=0)
    d_qkv = jnp.concatenate([d_q, d_k, d_v], axis=1).astype(jnp.bfloat16)
    g_qkv = product(a_one.T, d_qkv)
    d_a1 = product(d_qkv, qkv_w.T)
    g_ln1g = jnp.sum(d_a1 * normed_one, axis=0)
    g_ln1b = jnp.sum(d_a1, axis=0)
    d_x = d_h1 + norm_back(d_a1, normed_one, rstd_one, vecf[0])
    g_vec = jnp.stack([g_ln1g, g_ln1b, g_bq, g_bv, g_bout, g_ln2g, g_ln2b, g_bdown])
    return (d_x, (g_vec, g_bup, g_qkv, g_out, g_up, g_down))


def adamw(param, moments, grad, count):
    first = beta_one * moments[0] + (1.0 - beta_one) * grad
    second = beta_two * moments[1] + (1.0 - beta_two) * grad * grad
    corr_one = 1.0 - beta_one**count
    corr_two = 1.0 - beta_two**count
    update = first / corr_one / (jnp.sqrt(second / corr_two) + adam_eps) + decay_rate * param
    return (update, first, second)


def body(
    tokens,
    cotangent,
    lengths,
    vectors,
    bias_up,
    w_qkv,
    w_out,
    w_up,
    w_down,
    mom_vectors,
    mom_bias_up,
    mom_qkv,
    mom_out,
    mom_up,
    mom_down,
):
    params = (vectors, bias_up, w_qkv, w_out, w_up, w_down)
    moments = (mom_vectors, mom_bias_up, mom_qkv, mom_out, mom_up, mom_down)
    low = tuple((p.astype(jnp.bfloat16) for p in params))
    alibi = alibi_bias(MB_ROWS)
    place = jnp.arange(MB_ROWS)
    owned = tuple((jnp.zeros(p.shape, jnp.float32) for p in params))
    summed = None
    out_list = []
    dx_list = []
    for micro in range(MICRO):
        x_rows = tokens[micro * MB_ROWS : (micro + 1) * MB_ROWS]
        live = place < lengths[micro]
        grad_rows = jnp.where(
            live[:, None],
            cotangent[micro * MB_ROWS : (micro + 1) * MB_ROWS],
            jnp.zeros((), jnp.bfloat16),
        )
        ahead = (
            lax.all_gather(low[0], "dp", axis=1, tiled=True),
            lax.all_gather(low[1], "dp", axis=0, tiled=True),
            lax.all_gather(low[2], "dp", axis=0, tiled=True),
            lax.all_gather(low[3], "dp", axis=0, tiled=True),
            lax.all_gather(low[4], "dp", axis=0, tiled=True),
            lax.all_gather(low[5], "dp", axis=0, tiled=True),
        )
        out, saved = forward_block(x_rows, ahead, alibi)
        behind = (
            lax.all_gather(low[0], "dp", axis=1, tiled=True),
            lax.all_gather(low[1], "dp", axis=0, tiled=True),
            lax.all_gather(low[2], "dp", axis=0, tiled=True),
            lax.all_gather(low[3], "dp", axis=0, tiled=True),
            lax.all_gather(low[4], "dp", axis=0, tiled=True),
            lax.all_gather(low[5], "dp", axis=0, tiled=True),
        )
        d_x, grads = backward_block(saved, grad_rows, behind, alibi)
        out_list.append(out)
        dx_list.append(d_x)
        summed = grads if summed is None else tuple((a + b for a, b in zip(summed, grads)))
    owned = (
        lax.psum_scatter(summed[0], "dp", scatter_dimension=1, tiled=True),
        lax.psum_scatter(summed[1], "dp", scatter_dimension=0, tiled=True),
        lax.psum_scatter(summed[2], "dp", scatter_dimension=0, tiled=True),
        lax.psum_scatter(summed[3], "dp", scatter_dimension=0, tiled=True),
        lax.psum_scatter(summed[4], "dp", scatter_dimension=0, tiled=True),
        lax.psum_scatter(summed[5], "dp", scatter_dimension=0, tiled=True),
    )
    count = float(STEP)
    news = [adamw(p, m, g, count) for p, m, g in zip(params, moments, owned)]
    output = jnp.concatenate(out_list, axis=0)
    input_grad = jnp.concatenate(dx_list, axis=0)
    return (
        output,
        input_grad,
        owned[0],
        owned[1],
        owned[2],
        owned[3],
        owned[4],
        owned[5],
        news[0][0],
        news[1][0],
        news[2][0],
        news[3][0],
        news[4][0],
        news[5][0],
        news[0][1],
        news[1][1],
        news[2][1],
        news[3][1],
        news[4][1],
        news[5][1],
        news[0][2],
        news[1][2],
        news[2][2],
        news[3][2],
        news[4][2],
        news[5][2],
    )


def solution(mesh):
    in_specs = (
        P("dp", None),
        P("dp", None),
        P("dp"),
        P(None, "dp"),
        P("dp"),
        P("dp", None),
        P("dp", None),
        P("dp", None),
        P("dp", None),
        P(None, None, "dp"),
        P(None, "dp"),
        P(None, "dp", None),
        P(None, "dp", None),
        P(None, "dp", None),
        P(None, "dp", None),
    )
    out_specs = (
        P("dp", None),
        P("dp", None),
        P(None, "dp"),
        P("dp"),
        P("dp", None),
        P("dp", None),
        P("dp", None),
        P("dp", None),
        P(None, "dp"),
        P("dp"),
        P("dp", None),
        P("dp", None),
        P("dp", None),
        P("dp", None),
        P(None, "dp"),
        P("dp"),
        P("dp", None),
        P("dp", None),
        P("dp", None),
        P("dp", None),
        P(None, "dp"),
        P("dp"),
        P("dp", None),
        P("dp", None),
        P("dp", None),
        P("dp", None),
    )
    return jax.shard_map(body, mesh=mesh, in_specs=in_specs, out_specs=out_specs, check_vma=False)
```

profile of v0, /device:TPU:0, one launch (start us, length us, event | category | flops | bytes accessed | tf_op | source)
XLA Modules:
  0.0 1188.9 jit_solution(11100328769745039988)
XLA Ops:
  7.3 1.7 convert_element_type.173
  9.1 1.5 convert_element_type.182
  10.7 1.8 convert_element_type.184
  12.6 43.7 %all-gather = bf16[32,32,8]{1,2,0:T(8,128)(2,1)S(1)} all-gather(bf16[1,32,8]{1,2,0:T(8,128)(2,1)S(1)} %convert_bitcast_fusion), channel_id=1, replica_groups=mesh['dp'=32] {'dp'}, dimensions={0}, use_global_device_ids=true | all-gather | bytes 16896 | tf_op jit(solution)/shard_map/all_gather | solution.py:213
  56.5 37.0 %all-gather.1 = bf16[32,1,128]{2,1,0:T(2,128)(2,1)S(1)} all-gather(bf16[1,1,128]{2,1,0:T(2,128)(2,1)S(1)} %convert_bitcast_fusion.1), channel_id=1, replica_groups=mesh['dp'=32] {'dp'}, dimensions={0}, use_global_device_ids=true | all-gather | bytes 8448 | tf_op jit(solution)/shard_map/all_gather | solution.py:214
  94.7 1.2 iota_compare_fusion.1
  98.3 4.0 fusion.93
  108.4 33.4 %all-gather.9.cloned.1.call-done = bf16[1024,1024]{1,0:T(8,128)(2,1)} async-done(((bf16[32,1024]{1,0:T(8,128)(2,1)}), bf16[1024,1024]{1,0:T(8,128)(2,1)}) %all-gather.9.cloned.1.call-update) | async-done | bytes 2097168 | tf_op jit(solution)/shard_map/all_gather | solution.py:216
  141.9 2.2 fusion.112
  147.6 73.6 %all-gather.11.cloned.1.call-done = bf16[1024,4096]{1,0:T(8,128)(2,1)} async-done(((bf16[32,4096]{1,0:T(8,128)(2,1)}), bf16[1024,4096]{1,0:T(8,128)(2,1)}) %all-gather.11.cloned.1.call-update) | async-done | bytes 8388624 | tf_op jit(solution)/shard_map/all_gather | solution.py:217
  221.3 5.0 convolution_add_fusion.4
  226.4 2.4 fusion.95
  229.3 2.7 convolution_add_fusion.3
  232.0 10.4 convolution_add_fusion
  242.5 181.6 %reduce-scatter.14.cloned.1.call-done = f32[128,1024]{1,0:T(8,128)} async-done(((f32[4096,1024]{1,0:T(8,128)}), f32[128,1024]{1,0:T(8,128)}) %reduce-scatter.14.cloned.1.call-update) | async-done | bytes 524304 | tf_op jit(solution)/shard_map/reduce_scatter | solution.py:239
  424.2 3.2 multiply_add_fusion.2
  428.2 78.0 %all-gather.13.cloned.1.call-done = bf16[4096,1024]{1,0:T(8,128)(2,1)} async-done(((bf16[128,1024]{1,0:T(8,128)(2,1)}), bf16[4096,1024]{1,0:T(8,128)(2,1)}) %all-gather.13.cloned.1.call-update) | async-done | bytes 8388624 | tf_op jit(solution)/shard_map/all_gather | solution.py:218
  506.2 8.3 fusion.115
  514.5 4.3 fusion.114
  518.9 2.9 fusion.63
  521.9 3.7 multiply_reduce_fusion.1
  527.5 1.5 convolution_convert_fusion
  531.4 3.0 fusion.104
  534.8 1.2 fusion.25
  536.0 1.6 fusion.105
  537.6 1.5 convolution_convert_fusion.1
  539.1 1.2 copy.93
  541.5 2.4 fusion.106
  544.3 1.2 fusion.24
  546.5 2.8 fusion.80
  549.7 5.3 fusion.70
  555.3 4.0 fusion.54
  561.2 5.2 convolution_add_fusion.5
  567.5 2.0 fusion.71
  569.5 6.5 convolution_add_fusion.2
  577.1 3.7 fusion.65
  580.8 8.3 convolution_add_fusion.1
  589.9 39.6 %all-reduce = f32[4096]{0:T(1024)} all-reduce(f32[4096]{0:T(1024)S(1)} %add.398), channel_id=3, replica_groups=mesh['dp'=32] {'dp'}, use_global_device_ids=true, to_apply=%region_41.42.clone | all-reduce | flops 4096 | bytes 32768
  629.4 5.8 fusion.23
  635.3 5.1 fusion.22
  643.0 1.4 multiply_add_fusion.7
  644.4 51.4 %reduce-scatter.16.cloned.1.call-done = f32[32,8]{1,0:T(8,128)} async-done(((f32[1024,8]{1,0:T(8,128)}), f32[32,8]{1,0:T(8,128)}) %reduce-scatter.16.cloned.1.call-update) | async-done | bytes 1040
  697.3 140.2 %reduce-scatter.10.cloned.1.call-done = f32[32,1024]{1,0:T(8,128)} async-done(((f32[1024,1024]{1,0:T(8,128)}), f32[32,1024]{1,0:T(8,128)}) %reduce-scatter.10.cloned.1.call-update) | async-done | bytes 131088 | tf_op jit(solution)/shard_map/reduce_scatter | solution.py:237
  837.4 1.7 multiply_add_fusion.5
  839.1 155.7 %reduce-scatter.8.cloned.1.call-done = f32[32,3072]{1,0:T(8,128)} async-done(((f32[1024,3072]{1,0:T(8,128)}), f32[32,3072]{1,0:T(8,128)}) %reduce-scatter.8.cloned.1.call-update) | async-done | bytes 393232 | tf_op jit(solution)/shard_map/reduce_scatter | solution.py:236
  994.8 2.2 multiply_add_fusion.4
  997.0 182.5 %reduce-scatter.12.cloned.1.call-done = f32[32,4096]{1,0:T(8,128)} async-done(((f32[1024,4096]{1,0:T(8,128)}), f32[32,4096]{1,0:T(8,128)}) %reduce-scatter.12.cloned.1.call-update) | async-done | bytes 524304 | tf_op jit(solution)/shard_map/reduce_scatter | solution.py:238
  1179.5 2.4 multiply_add_fusion.3
  (357 shorter events, 30.7 us)
Async XLA Ops:
  7.2 49.2 %copy-start.117 = (f32[128]{0:T(128)S(1)}, f32[128]{0:T(128)}, u32[]{:S(2)}) copy-start(f32[128]{0:T(128)} %param.19) | copy-start | bytes 1540
  7.2 86.9 %copy-start.115 = (s32[2]{0:T(128)S(1)}, s32[2]{0:T(128)}, u32[]{:S(2)}) copy-start(s32[2]{0:T(128)} %param.17) | copy-start | bytes 28
  7.2 89.9 %copy-start.2 = (bf16[256,1024]{1,0:T(8,128)(2,1)S(1)}, bf16[256,1024]{1,0:T(8,128)(2,1)}, u32[]{:S(2)}) copy-start(bf16[256,1024]{1,0:T(8,128)(2,1)} %param.15) | copy-start | bytes 1572868
  7.2 91.0 %all-gather.7.cloned.1.call-start = ((), (), s32[]{:S(2)}) async-start(), calls=%async_computation.5 | async-start | bytes 6488064 | tf_op jit(solution)/shard_map/all_gather | solution.py:215
  9.1 132.8 %all-gather.9.cloned.1.call-start = ((), (), s32[]{:S(2)}) async-start(), calls=%async_computation.6 | async-start | bytes 2162688 | tf_op jit(solution)/shard_map/all_gather | solution.py:216
  10.7 210.5 %all-gather.11.cloned.1.call-start = ((), (), s32[]{:S(2)}) async-start(), calls=%async_computation.7 | async-start | bytes 8650752 | tf_op jit(solution)/shard_map/all_gather | solution.py:217
  12.5 411.6 %reduce-scatter.14.cloned.1.call-start = ((), (), s32[]{:S(2)}) async-start(), calls=%async_computation.12 | async-start | bytes 17301504 | tf_op jit(solution)/shard_map/reduce_scatter | solution.py:239
  94.2 12.5 %copy-start.124 = (f32[16]{0:T(128)}, f32[16]{0:T(128)S(1)}, u32[]{:S(2)}) copy-start(f32[16]{0:T(128)S(1)} %exponential_negate_fusion) | copy-start | bytes 196
  97.1 9.6 copy-start.98
  97.1 9.6 copy-start.64
  98.3 43.6 %copy-start.66 = (f32[1,1024]{1,0:T(1,128)}, f32[1,1024]{1,0:T(1,128)S(1)}, u32[]{:S(2)}) copy-start(f32[1,1024]{1,0:T(1,128)S(1)} %get-tuple-element.93) | copy-start | bytes 12292
  104.5 40.5 %copy-start.31 = (bf16[128,1024]{0,1:T(8,128)(2,1)}, bf16[128,1024]{0,1:T(8,128)(2,1)S(1)}, u32[]{:S(2)}) copy-start(bf16[128,1024]{0,1:T(8,128)(2,1)S(1)} %copy.89) | copy-start | bytes 786436
  108.4 36.4 %copy-start.27 = (bf16[16,64,128]{2,1,0:T(8,128)(2,1)}, bf16[16,64,128]{2,1,0:T(8,128)(2,1)S(1)}, u32[]{:S(2)}) copy-start(bf16[16,64,128]{2,1,0:T(8,128)(2,1)S(1)} %convolution_convert_fusion.3) | copy-start | bytes 786436
  108.4 35.9 %copy-start.50 = (bf16[128,1024]{0,1:T(8,128)(2,1)S(1)}, bf16[128,1024]{0,1:T(8,128)(2,1)}, u32[]{:S(2)}) copy-start(bf16[128,1024]{0,1:T(8,128)(2,1)} %copy.91) | copy-start | bytes 786436
  144.1 77.2 %copy-start.72 = (f32[128]{0:T(128)}, f32[128]{0:T(128)S(1)}, u32[]{:S(2)}) copy-start(f32[128]{0:T(128)S(1)} %broadcast_multiply_fusion.10) | copy-start | bytes 1540
  145.9 75.4 %copy-start.25 = (bf16[16,64,128]{2,1,0:T(8,128)(2,1)}, bf16[16,64,128]{2,1,0:T(8,128)(2,1)S(1)}, u32[]{:S(2)}) copy-start(bf16[16,64,128]{2,1,0:T(8,128)(2,1)S(1)} %convolution_convert_fusion.2) | copy-start | bytes 786436
  145.9 75.4 %copy-start.60 = (f32[32,1,128]{2,1,0:T(1,128)S(1)}, f32[32,1,128]{2,1,0:T(1,128)}, u32[]{:S(2)}) copy-start(f32[32,1,128]{2,1,0:T(1,128)} %convert_element_type.216) | copy-start | bytes 49156
  146.9 74.3 %copy-start.75 = (f32[128]{0:T(128)}, f32[128]{0:T(128)S(1)}, u32[]{:S(2)}) copy-start(f32[128]{0:T(128)S(1)} %broadcast_multiply_fusion.8) | copy-start | bytes 1540
  147.1 74.1 %copy-start.84 = (f32[128]{0:T(128)}, f32[128]{0:T(128)S(1)}, u32[]{:S(2)}) copy-start(f32[128]{0:T(128)S(1)} %add_rsqrt_fusion.2) | copy-start | bytes 1540
  221.3 7.6 slice-start
  242.5 185.0 %copy-start.20 = (bf16[256,1024]{1,0:T(8,128)(2,1)S(1)}, bf16[256,1024]{1,0:T(8,128)(2,1)}, u32[]{:S(2)}) copy-start(bf16[256,1024]{1,0:T(8,128)(2,1)} %param.16) | copy-start | bytes 1572868
  242.5 185.0 %copy-start.111 = (pred[128]{0:T(512)(128)(4,1)S(1)}, pred[128]{0:T(512)(128)(4,1)}, u32[]{:S(2)}) copy-start(pred[128]{0:T(512)(128)(4,1)} %iota_compare_fusion) | copy-start | bytes 388
  242.5 184.9 %copy-start.113 = (pred[128]{0:T(512)(128)(4,1)S(1)}, pred[128]{0:T(512)(128)(4,1)}, u32[]{:S(2)}) copy-start(pred[128]{0:T(512)(128)(4,1)} %iota_compare_fusion.1) | copy-start | bytes 388
  242.5 263.7 %all-gather.13.cloned.1.call-start = ((), (), s32[]{:S(2)}) async-start(), calls=%async_computation.8 | async-start | bytes 8650752 | tf_op jit(solution)/shard_map/all_gather | solution.py:218
  427.4 268.5 %reduce-scatter.16.cloned.1.call-start = ((), (), s32[]{:S(2)}) async-start(), calls=%async_computation.13 | async-start | bytes 540672
  506.2 8.3 copy-start.12
  506.2 8.3 copy-start.119
  506.2 12.6 %slice-start.2 = ((s8[8388608]{0:T(1024)(128)(4,1)}), s8[4194304]{0:T(1024)(128)(4,1)S(1)}, s32[]{:S(2)}) async-start(s8[8388608]{0:T(1024)(128)(4,1)} %bitcast.154), calls=%async_computation.16 | async-start | bytes 8388608
  526.7 10.9 copy-start.14
  546.5 8.5 slice-start.4
  561.2 276.2 %reduce-scatter.10.cloned.1.call-start = ((), (), s32[]{:S(2)}) async-start(), calls=%async_computation.10 | async-start | bytes 4325376 | tf_op jit(solution)/shard_map/reduce_scatter | solution.py:237
  566.5 428.3 %reduce-scatter.8.cloned.1.call-start = ((), (), s32[]{:S(2)}) async-start(), calls=%async_computation.9 | async-start | bytes 12976128 | tf_op jit(solution)/shard_map/reduce_scatter | solution.py:236
  576.1 603.4 %reduce-scatter.12.cloned.1.call-start = ((), (), s32[]{:S(2)}) async-start(), calls=%async_computation.11 | async-start | bytes 17301504 | tf_op jit(solution)/shard_map/reduce_scatter | solution.py:238
  589.1 40.3 %copy-start.114 = (f32[1,1024]{1,0:T(1,128)S(1)}, f32[1,1024]{1,0:T(1,128)}, u32[]{:S(2)}) copy-start(f32[1,1024]{1,0:T(1,128)} %get-tuple-element.91) | copy-start | bytes 12292
  635.3 6.1 copy-start.16
  635.3 6.1 copy-start.18
  635.3 6.1 copy-start.56
  635.3 6.1 copy-start.57
  635.3 6.1 copy-start.105
  641.4 55.2 %copy-start.97 = (f32[8,32]{1,0:T(8,128)S(1)}, f32[8,32]{1,0:T(8,128)}, u32[]{:S(2)}) copy-start(f32[8,32]{1,0:T(8,128)} %param.18) | copy-start | bytes 3076
  641.4 55.2 %copy-start.110 = (f32[2,8,32]{2,1,0:T(8,128)S(1)}, f32[2,8,32]{2,1,0:T(8,128)}, u32[]{:S(2)}) copy-start(f32[2,8,32]{2,1,0:T(8,128)} %param.24) | copy-start | bytes 6148
  641.4 196.0 %copy-start.58 = (f32[32,1024]{1,0:T(8,128)S(1)}, f32[32,1024]{1,0:T(8,128)}, u32[]{:S(2)}) copy-start(f32[32,1024]{1,0:T(8,128)} %param.21) | copy-start | bytes 393220
  641.9 195.5 %copy-start.59 = (f32[2,32,1024]{2,1,0:T(8,128)S(1)}, f32[2,32,1024]{2,1,0:T(8,128)}, u32[]{:S(2)}) copy-start(f32[2,32,1024]{2,1,0:T(8,128)} %param.27) | copy-start | bytes 786436
  641.9 352.9 %copy-start.34 = (f32[32,3072]{1,0:T(8,128)S(1)}, f32[32,3072]{1,0:T(8,128)}, u32[]{:S(2)}) copy-start(f32[32,3072]{1,0:T(8,128)} %param.20) | copy-start | bytes 1179652
  641.9 352.9 %copy-start.54 = (f32[2,32,3072]{2,1,0:T(8,128)S(1)}, f32[2,32,3072]{2,1,0:T(8,128)}, u32[]{:S(2)}) copy-start(f32[2,32,3072]{2,1,0:T(8,128)} %param.26) | copy-start | bytes 2359300
  643.0 536.5 %copy-start.33 = (f32[32,4096]{1,0:T(8,128)S(1)}, f32[32,4096]{1,0:T(8,128)}, u32[]{:S(2)}) copy-start(f32[32,4096]{1,0:T(8,128)} %param.22) | copy-start | bytes 1572868
  643.0 536.5 %copy-start.39 = (f32[2,32,4096]{2,1,0:T(8,128)S(1)}, f32[2,32,4096]{2,1,0:T(8,128)}, u32[]{:S(2)}) copy-start(f32[2,32,4096]{2,1,0:T(8,128)} %param.28) | copy-start | bytes 3145732
  696.6 485.3 %copy-start.95 = (f32[8,32]{1,0:T(8,128)}, f32[8,32]{1,0:T(8,128)S(1)}, u32[]{:S(2)}) copy-start(f32[8,32]{1,0:T(8,128)S(1)} %copy.114) | copy-start | bytes 3076
  (93 other events, 330.2 us)
Sparse Core Ops, SparseCore 0:
  11.5 72.0 all-gather.6
  87.0 54.8 all-gather.8
  145.3 75.8 all-gather.10
  242.6 181.5 reduce-scatter.13
  427.5 78.7 all-gather.12
  561.3 134.4 reduce-scatter.15
  698.7 138.6 reduce-scatter.9
  844.0 150.7 reduce-scatter.7
  997.7 181.7 reduce-scatter.11
where the time goes:
time: 1200 us; the launch traced here: 1190 us
  waiting for transfers between devices  897 us (75%)
  blocking collectives  120 us (10%)
  matrix products  112 us (9%)
  other arithmetic  27.9 us (2%)
  between operations  16 us (1%)
  local copies, waits for them, and re-layouts  15.7 us (1%)
    reduce_scatter x1, waiting for transfers between devices, body(): lax.psum_scatter(summed[4], 'dp', scatter_dimension=0, tiled=True)  183 us
    reduce_scatter x1, waiting for transfers between devices, body(): lax.psum_scatter(summed[5], 'dp', scatter_dimension=0, tiled=True)  182 us
    reduce_scatter x1, waiting for transfers between devices, body(): lax.psum_scatter(summed[2], 'dp', scatter_dimension=0, tiled=True)  156 us
    reduce_scatter x1, waiting for transfers between devices, body(): lax.psum_scatter(summed[3], 'dp', scatter_dimension=0, tiled=True)  140 us
    dot_general x24, matrix products, product(): return jnp.dot(left, right, preferred_element_type=jnp.float32)  99.2 us
    all_gather x1, waiting for transfers between devices, body(): lax.all_gather(low[5], 'dp', axis=0, tiled=True)  78 us
    all_gather x1, waiting for transfers between devices, body(): lax.all_gather(low[4], 'dp', axis=0, tiled=True)  73.6 us
    unnamed x10, waiting for transfers between devices  51.6 us
  transfers between devices with their start and end apart: 9, of which 8 were waited for; matrix products, arithmetic and copies ran while one was open for 6% of the time, Pallas kernels for 0%

commit v1 on v0

--- a/solution.py
+++ b/solution.py
@@ -1,8 +1,11 @@
+import functools
 import math
 
 import jax
 import jax.numpy as jnp
 from jax import lax
+from jax.experimental import pallas as pl
+from jax.experimental.pallas import tpu as pltpu
 from jax.sharding import PartitionSpec as P
 
 D = 1024
@@ -175,6 +178,212 @@
     return (update, first, second)
 
 
+MESH_ID = pl.DeviceIdType.MESH
+
+
+def grid_of(count):
+    known = {32: (4, 2, 2), 128: (4, 4, 4)}
+    return known.get(count, (count // 2,))
+
+
+def locate(me, sizes):
+    rest, coords = me // 2, []
+    for size in reversed(sizes):
+        coords.append(rest % size)
+        rest = rest // size
+    return tuple(reversed(coords)), me % 2
+
+
+def device_at(coords, core, sizes):
+    index = 0
+    for value, size in zip(coords, sizes):
+        index = index * size + value
+    return index * 2 + core
+
+
+def swapped(coords, dim, value):
+    return tuple(value if at == dim else old for at, old in enumerate(coords))
+
+
+def neighbours(coords, core, sizes):
+    found = [device_at(coords, 1 - core, sizes)]
+    for dim, size in enumerate(sizes):
+        for step in range(1, size):
+            found.append(device_at(swapped(coords, dim, (coords[dim] + step) % size), core, sizes))
+    return found
+
+
+def greet(others):
+    barrier = pltpu.get_barrier_semaphore()
+    for other in others:
+        pl.semaphore_signal(barrier, inc=1, device_id=(other,), device_id_type=MESH_ID)
+    pl.semaphore_wait(barrier, len(others))
+
+
+class Sems:
+    def __init__(self, send, recv):
+        self.send, self.recv, self.used = send, recv, 0
+
+    def pair(self):
+        at = self.used
+        self.used += 1
+        return self.send.at[at], self.recv.at[at]
+
+
+def remote(sems, src, dst, target):
+    send_sem, recv_sem = sems.pair()
+    copy = pltpu.make_async_remote_copy(
+        src_ref=src, dst_ref=dst, send_sem=send_sem, recv_sem=recv_sem,
+        device_id=(target,), device_id_type=MESH_ID,
+    )
+    copy.start()
+    return copy
+
+
+class Gather:
+    def __init__(self, full, colours, sizes, coords, core, sems):
+        self.full, self.colours, self.sizes = full, colours, sizes
+        self.coords, self.core, self.sems = coords, core, sems
+        self.axis = [[] for _ in colours]
+        self.swap = []
+        self.sent = []
+
+    def view(self, colour, fixed):
+        start, width, _ = colour
+        place = tuple(fixed.get(dim, slice(None)) for dim in range(len(self.sizes)))
+        return self.full.at[(*place, self.core, slice(None), pl.ds(start, width))]
+
+    def start(self, stage, own=None):
+        for at, colour in enumerate(self.colours):
+            order = colour[2]
+            dim = order[stage]
+            fixed = {d: self.coords[d] for d in order[stage:]}
+            held = self.view(colour, fixed)
+            source = held if own is None else own.at[:, pl.ds(colour[0], colour[1])]
+            self.axis[at] = []
+            for step in range(1, self.sizes[dim]):
+                peer = swapped(self.coords, dim, (self.coords[dim] + step) % self.sizes[dim])
+                self.axis[at].append(remote(self.sems, source, held, device_at(peer, self.core, self.sizes)))
+            self.sent += self.axis[at]
+
+    def land(self, stage):
+        partner = device_at(self.coords, 1 - self.core, self.sizes)
+        for at, colour in enumerate(self.colours):
+            order = colour[2]
+            dim = order[stage]
+            for copy in self.axis[at]:
+                copy.wait_recv()
+            fixed = {d: self.coords[d] for d in order[stage + 1:]}
+            if stage == 0:
+                views = [self.view(colour, fixed)]
+            else:
+                views = [
+                    self.view(colour, {**fixed, dim: (self.coords[dim] + step) % self.sizes[dim]})
+                    for step in range(1, self.sizes[dim])
+                ]
+            for view in views:
+                self.swap.append(remote(self.sems, view, view, partner))
+
+    def finish(self):
+        for copy in self.swap:
+            copy.wait_recv()
+
+    def drain(self):
+        for copy in self.sent + self.swap:
+            copy.wait_send()
+
+
+def colours_of(columns, sizes):
+    last = len(sizes) - 1
+    if last < 2:
+        return [(0, columns, tuple(range(len(sizes))))]
+    tiles = columns // 128
+    if tiles < 8:
+        return [(0, columns, (0, 1, 2))]
+    third = max(1, tiles // 8)
+    first = (tiles - third) // 2
+    second = tiles - third - first
+    return [
+        (0, first * 128, (0, 1, 2)),
+        (first * 128, second * 128, (0, 2, 1)),
+        ((first + second) * 128, third * 128, (2, 1, 0)),
+    ]
+
+
+def gather_kernel(sizes, count, *refs):
+    shards, fulls = refs[:count], refs[count : 2 * count]
+    owns = refs[2 * count : 3 * count]
+    send_sem, recv_sem, local_sem = refs[3 * count :]
+    coords, core = locate(lax.axis_index("dp"), sizes)
+    for shard, own in zip(shards, owns):
+        own[...] = shard[...].astype(own.dtype)
+    greet(neighbours(coords, core, sizes))
+    sems = Sems(send_sem, recv_sem)
+    items = [
+        Gather(full, colours_of(full.shape[-1], sizes), sizes, coords, core, sems) for full in fulls
+    ]
+    local = []
+    for at, (own, full) in enumerate(zip(owns, fulls)):
+        copy = pltpu.make_async_copy(own, full.at[(*coords, core)], local_sem.at[at])
+        copy.start()
+        local.append(copy)
+    stages = len(sizes)
+    items[0].start(0, owns[0])
+    for turn in range(count + stages):
+        for stage in range(stages):
+            at = turn - stage
+            if 0 <= at < count:
+                if stage == 0:
+                    if at + 1 < count:
+                        items[at + 1].start(0, owns[at + 1])
+                    local[at].wait()
+                items[at].land(stage)
+                if stage + 1 < stages:
+                    items[at].start(stage + 1)
+        at = turn - stages
+        if 0 <= at < count:
+            items[at].finish()
+    for item in items:
+        item.drain()
+
+
+def gather_all(shards, count):
+    sizes = grid_of(count)
+    copies = 400
+    n = len(shards)
+    fulls = pl.pallas_call(
+        functools.partial(gather_kernel, sizes, n),
+        out_shape=[jax.ShapeDtypeStruct((*sizes, 2, *s.shape), jnp.bfloat16) for s in shards],
+        in_specs=[pl.BlockSpec(memory_space=pltpu.VMEM)] * n,
+        out_specs=[pl.BlockSpec(memory_space=pltpu.HBM)] * n,
+        scratch_shapes=[pltpu.VMEM(s.shape, jnp.bfloat16) for s in shards]
+        + [pltpu.SemaphoreType.DMA((copies,)), pltpu.SemaphoreType.DMA((copies,)), pltpu.SemaphoreType.DMA((n,))],
+        compiler_params=pltpu.CompilerParams(collective_id=0, has_side_effects=True),
+        name="gather_all",
+    )(*shards)
+    return [full.reshape(-1, *full.shape[-2:]) for full in fulls]
+
+
+def small_block(vectors, bias_up, me):
+    wide = jnp.zeros((8, 128), jnp.float32)
+    width = vectors.shape[1]
+    per = 128 // width
+    wide = lax.dynamic_update_slice(wide, vectors, (0, (me % per) * width))
+    tail = jnp.zeros((8, 128), jnp.float32)
+    span = bias_up.shape[0]
+    tail = lax.dynamic_update_slice(tail, bias_up[None, :], (0, (me % (128 // span)) * span))
+    return jnp.concatenate([wide, tail], axis=0)
+
+
+def small_parts(small, vectors, bias_up):
+    per = 128 // vectors.shape[1]
+    span = 128 // bias_up.shape[0]
+    n = small.shape[0]
+    vec = jnp.sum(small[:, :8].astype(jnp.float32).reshape(n // per, per, 8, 128), axis=1)
+    bias = jnp.sum(small[:, 8].astype(jnp.float32).reshape(n // span, span, 128), axis=1)
+    return vec.transpose(1, 0, 2).reshape(8, -1).astype(jnp.bfloat16), bias.reshape(-1).astype(jnp.bfloat16)
+
+
 def body(
     tokens,
     cotangent,
@@ -194,7 +403,20 @@
 ):
     params = (vectors, bias_up, w_qkv, w_out, w_up, w_down)
     moments = (mom_vectors, mom_bias_up, mom_qkv, mom_out, mom_up, mom_down)
-    low = tuple((p.astype(jnp.bfloat16) for p in params))
+    me = lax.axis_index("dp")
+    count = lax.axis_size("dp")
+    small, full_out, full_qkv, full_up, full_down = gather_all(
+        [small_block(vectors, bias_up, me), w_out, w_qkv, w_up, w_down], count
+    )
+    vec_low, bias_low = small_parts(small, vectors, bias_up)
+    weights = (
+        vec_low,
+        bias_low,
+        full_qkv.reshape(-1, w_qkv.shape[1]),
+        full_out.reshape(-1, w_out.shape[1]),
+        full_up.reshape(-1, w_up.shape[1]),
+        full_down.reshape(-1, w_down.shape[1]),
+    )
     alibi = alibi_bias(MB_ROWS)
     place = jnp.arange(MB_ROWS)
     owned = tuple((jnp.zeros(p.shape, jnp.float32) for p in params))
@@ -209,24 +431,8 @@
             cotangent[micro * MB_ROWS : (micro + 1) * MB_ROWS],
             jnp.zeros((), jnp.bfloat16),
         )
-        ahead = (
-            lax.all_gather(low[0], "dp", axis=1, tiled=True),
-            lax.all_gather(low[1], "dp", axis=0, tiled=True),
-            lax.all_gather(low[2], "dp", axis=0, tiled=True),
-            lax.all_gather(low[3], "dp", axis=0, tiled=True),
-            lax.all_gather(low[4], "dp", axis=0, tiled=True),
-            lax.all_gather(low[5], "dp", axis=0, tiled=True),
-        )
-        out, saved = forward_block(x_rows, ahead, alibi)
-        behind = (
-            lax.all_gather(low[0], "dp", axis=1, tiled=True),
-            lax.all_gather(low[1], "dp", axis=0, tiled=True),
-            lax.all_gather(low[2], "dp", axis=0, tiled=True),
-            lax.all_gather(low[3], "dp", axis=0, tiled=True),
-            lax.all_gather(low[4], "dp", axis=0, tiled=True),
-            lax.all_gather(low[5], "dp", axis=0, tiled=True),
-        )
-        d_x, grads = backward_block(saved, grad_rows, behind, alibi)
+        out, saved = forward_block(x_rows, weights, alibi)
+        d_x, grads = backward_block(saved, grad_rows, weights, alibi)
         out_list.append(out)
         dx_list.append(d_x)
         summed = grads if summed is None else tuple((a + b for a, b in zip(summed, grads)))

time: 1200 us -> 1070 us (0.89)
  waiting for transfers between devices: 897 us -> 704 us
  Pallas kernels: 0 us -> 147 us
  blocking collectives: 120 us -> 41.7 us
    all_gather x4 -> x0, waiting for transfers between devices: 185 us -> none  [the longest x1 78 us: body(): lax.all_gather(low[5], 'dp', axis=0, tiled=True)]
    pallas_call x0 -> x1, Pallas kernels: none -> 147 us  [gather_all(): pl.pallas_call(functools.partial(gather_kernel, sizes, n), out_shape=[jax...]
    all_gather x2 -> x0, blocking collectives: 80.8 us -> none  [the longest x1 43.7 us: body(): lax.all_gather(low[0], 'dp', axis=1, tiled=True)]
    unnamed x10 -> x6, waiting for transfers between devices: 51.6 us -> 40.1 us
  transfers between devices with their start and end apart: 9 -> 5, of which waited for: 8 -> 5; matrix products, arithmetic and copies ran while one was open for 6% -> 6% of each run, Pallas kernels for 0% -> 0%
where the time goes in v1:
time: 1070 us; the launch traced here: 1060 us
  waiting for transfers between devices  704 us (66%)
  Pallas kernels  147 us (14%)
  matrix products  109 us (10%)
  blocking collectives  41.7 us (4%)
  other arithmetic  22.6 us (2%)
  local copies, waits for them, and re-layouts  18.1 us (2%)
  between operations  15.5 us (1%)
    reduce_scatter x1, waiting for transfers between devices, body(): lax.psum_scatter(summed[5], 'dp', scatter_dimension=0, tiled=True)  185 us
    reduce_scatter x1, waiting for transfers between devices, body(): lax.psum_scatter(summed[4], 'dp', scatter_dimension=0, tiled=True)  182 us
    reduce_scatter x1, waiting for transfers between devices, body(): lax.psum_scatter(summed[2], 'dp', scatter_dimension=0, tiled=True)  156 us
    pallas_call x1, Pallas kernels, gather_all(): pl.pallas_call(functools.partial(gather_kernel, sizes, n), out_shape=[jax...  147 us
    reduce_scatter x1, waiting for transfers between devices, body(): lax.psum_scatter(summed[3], 'dp', scatter_dimension=0, tiled=True)  141 us
    dot_general x24, matrix products, product(): return jnp.dot(left, right, preferred_element_type=jnp.float32)  94.7 us
    unnamed x1, blocking collectives  41.7 us
    unnamed x6, waiting for transfers between devices  40.1 us
  transfers between devices with their start and end apart: 5, of which 5 were waited for; matrix products, arithmetic and copies ran while one was open for 6% of the time, Pallas kernels for 0%

profile of v1, /device:TPU:0, one launch (start us, length us, event | category | flops | bytes accessed | tf_op | source)
XLA Modules:
  0.0 1057.7 jit_solution(16233023424816096180)
XLA Ops:
  8.2 1.3 select_maximum_fusion.refs_0_
  9.4 147.0 %gather_all.1 = (bf16[4,2,2,2,16,128]{5,4,3,2,1,0:T(8,128)(2,1)}, bf16[4,2,2,2,32,1024]{5,4,3,2,1,0:T(8,128)(2,1)}, bf16[4,2,2,2,32,3072]{5,4,3,2,1,0:T(8,128)(2...) custom-call(f32[16,128]{1,0:T(8,128)} %select_maximum_fusion.refs_0_, f32[32,1024]{1,0:T(8,128)} %refs_1_.1, ...), custom_call_target="tpu_custom_call" | custom-call | tf_op jit(solution)/shard_map/gather_all/pallas_call | solution.py:354
  159.3 4.0 fusion.93
  170.1 1.1 copy.83
  171.2 1.9 copy.84
  173.1 1.8 copy.85
  174.9 1.4 fusion.112
  177.7 5.4 convolution_add_fusion.3
  183.2 1.3 convolution_add_fusion.4
  185.2 1.3 iota_compare_fusion.1
  186.6 7.2 fusion.115
  193.8 2.9 fusion.63
  196.7 6.9 fusion.114
  203.7 3.1 multiply_reduce_fusion.1
  206.9 1.3 fusion.103
  208.9 1.5 convolution_convert_fusion
  210.5 1.1 copy.96
  211.6 1.2 multiply_reduce_fusion.2
  212.8 2.4 fusion.104
  215.7 1.2 fusion.25
  216.8 1.2 fusion.105
  218.0 1.5 convolution_convert_fusion.1
  219.5 1.1 copy.91
  221.8 2.4 fusion.106
  224.2 1.8 fusion.14
  226.1 1.2 fusion.24
  228.8 5.3 fusion.70
  234.2 3.7 fusion.54
  239.2 1.8 fusion.80
  241.0 2.6 convolution_add_fusion.5
  244.8 2.0 fusion.71
  246.8 6.4 convolution_add_fusion.2
  254.2 3.8 fusion.65
  258.0 8.2 convolution_add_fusion.1
  267.3 4.0 fusion.95
  271.3 9.8 convolution_add_fusion
  281.1 41.7 %all-reduce.1 = f32[4096]{0:T(1024)S(1)} all-reduce(f32[4096]{0:T(1024)S(1)} %add.411), channel_id=3, replica_groups=mesh['dp'=32] {'dp'}, use_global_device_ids=true, to_apply=%region_42.43.clone | all-reduce | flops 4096 | bytes 32768
  322.8 5.7 fusion.23
  328.7 5.1 fusion.22
  337.0 40.0 %reduce-scatter.16.cloned.1.call-done = f32[32,8]{1,0:T(8,128)} async-done(((f32[1024,8]{1,0:T(8,128)}), f32[32,8]{1,0:T(8,128)}) %reduce-scatter.16.cloned.1.call-update) | async-done | bytes 1040
  378.4 140.6 %reduce-scatter.10.cloned.1.call-done = f32[32,1024]{1,0:T(8,128)} async-done(((f32[1024,1024]{1,0:T(8,128)}), f32[32,1024]{1,0:T(8,128)}) %reduce-scatter.10.cloned.1.call-update) | async-done | bytes 131088 | tf_op jit(solution)/shard_map/reduce_scatter | solution.py:443
  519.0 1.7 multiply_add_fusion.5
  520.7 155.7 %reduce-scatter.8.cloned.1.call-done = f32[32,3072]{1,0:T(8,128)} async-done(((f32[1024,3072]{1,0:T(8,128)}), f32[32,3072]{1,0:T(8,128)}) %reduce-scatter.8.cloned.1.call-update) | async-done | bytes 393232 | tf_op jit(solution)/shard_map/reduce_scatter | solution.py:442
  676.4 2.2 multiply_add_fusion.4
  678.6 182.4 %reduce-scatter.12.cloned.1.call-done = f32[32,4096]{1,0:T(8,128)} async-done(((f32[1024,4096]{1,0:T(8,128)}), f32[32,4096]{1,0:T(8,128)}) %reduce-scatter.12.cloned.1.call-update) | async-done | bytes 524304 | tf_op jit(solution)/shard_map/reduce_scatter | solution.py:444
  861.0 2.4 multiply_add_fusion.3
  863.4 185.0 %reduce-scatter.14.cloned.1.call-done = f32[128,1024]{1,0:T(8,128)} async-done(((f32[4096,1024]{1,0:T(8,128)}), f32[128,1024]{1,0:T(8,128)}) %reduce-scatter.14.cloned.1.call-update) | async-done | bytes 524304 | tf_op jit(solution)/shard_map/reduce_scatter | solution.py:445
  1048.4 2.4 multiply_add_fusion.2
  (237 shorter events, 25.0 us)
Async XLA Ops:
  7.2 151.6 %copy-start.1 = (bf16[256,1024]{1,0:T(8,128)(2,1)S(1)}, bf16[256,1024]{1,0:T(8,128)(2,1)}, u32[]{:S(2)}) copy-start(bf16[256,1024]{1,0:T(8,128)(2,1)} %param.15) | copy-start | bytes 1572868
  7.2 369.8 %reduce-scatter.16.cloned.1.call-start = ((), (), s32[]{:S(2)}) async-start(), calls=%async_computation.9 | async-start | bytes 540672
  158.9 4.4 slice-start.2
  159.2 4.1 copy-start.57
  159.2 4.4 slice-start.3
  171.2 5.6 copy-start.27
  176.9 6.2 slice-start
  177.4 29.4 %copy-start.2 = (f32[128,1024]{1,0:T(8,128)}, f32[128,1024]{1,0:T(8,128)S(1)}, u32[]{:S(2)}) copy-start(f32[128,1024]{1,0:T(8,128)S(1)} %get-tuple-element.122) | copy-start | bytes 1572868
  177.7 5.5 slice-start.1
  184.5 12.2 %copy-start.8 = (f32[128,4096]{1,0:T(8,128)}, f32[128,4096]{1,0:T(8,128)S(1)}, u32[]{:S(2)}) copy-start(f32[128,4096]{1,0:T(8,128)S(1)} %convolution_add_fusion.4) | copy-start | bytes 6291460
  186.5 41.7 %copy-start.61 = (pred[128]{0:T(512)(128)(4,1)}, pred[128]{0:T(512)(128)(4,1)S(1)}, u32[]{:S(2)}) copy-start(pred[128]{0:T(512)(128)(4,1)S(1)} %get-tuple-element.135) | copy-start | bytes 388
  186.6 41.7 %copy-start.63 = (pred[128]{0:T(512)(128)(4,1)}, pred[128]{0:T(512)(128)(4,1)S(1)}, u32[]{:S(2)}) copy-start(pred[128]{0:T(512)(128)(4,1)S(1)} %get-tuple-element.136) | copy-start | bytes 388
  220.6 5.4 copy-start.48
  221.7 5.5 copy-start.47
  224.2 9.9 slice-start.4
  228.7 5.4 slice-start.5
  228.8 5.4 copy-start.37
  228.8 5.4 copy-start.39
  228.8 5.4 copy-start.41
  228.8 5.4 copy-start.58
  228.8 5.4 copy-start.60
  234.2 4.9 copy-start.24
  239.1 279.9 %reduce-scatter.10.cloned.1.call-start = ((), (), s32[]{:S(2)}) async-start(), calls=%async_computation.6 | async-start | bytes 4325376 | tf_op jit(solution)/shard_map/reduce_scatter | solution.py:443
  243.7 432.7 %reduce-scatter.8.cloned.1.call-start = ((), (), s32[]{:S(2)}) async-start(), calls=%async_computation.5 | async-start | bytes 12976128 | tf_op jit(solution)/shard_map/reduce_scatter | solution.py:442
  253.2 607.8 %reduce-scatter.12.cloned.1.call-start = ((), (), s32[]{:S(2)}) async-start(), calls=%async_computation.7 | async-start | bytes 17301504 | tf_op jit(solution)/shard_map/reduce_scatter | solution.py:444
  266.3 5.0 copy-start.62
  266.3 782.1 %reduce-scatter.14.cloned.1.call-start = ((), (), s32[]{:S(2)}) async-start(), calls=%async_computation.8 | async-start | bytes 17301504 | tf_op jit(solution)/shard_map/reduce_scatter | solution.py:445
  281.1 41.7 %copy-start.66 = (f32[1,8,128]{2,0,1:T(1,128)S(1)}, f32[1,8,128]{2,0,1:T(1,128)}, u32[]{:S(2)}) copy-start(f32[1,8,128]{2,0,1:T(1,128)} %get-tuple-element.100) | copy-start | bytes 12292
  322.8 5.7 copy-start.9
  328.6 6.1 copy-start.73
  328.6 6.1 copy-start.72
  328.6 6.1 copy-start.71
  328.6 6.1 copy-start.70
  328.6 6.1 copy-start.11
  328.6 6.1 copy-start.14
  328.6 6.1 copy-start.51
  328.7 6.1 copy-start.52
  334.8 43.0 %copy-start.56 = (f32[8,32]{1,0:T(8,128)S(1)}, f32[8,32]{1,0:T(8,128)}, u32[]{:S(2)}) copy-start(f32[8,32]{1,0:T(8,128)} %param.18) | copy-start | bytes 3076
  334.8 43.0 %copy-start.65 = (f32[2,8,32]{2,1,0:T(8,128)S(1)}, f32[2,8,32]{2,1,0:T(8,128)}, u32[]{:S(2)}) copy-start(f32[2,8,32]{2,1,0:T(8,128)} %param.24) | copy-start | bytes 6148
  334.8 184.2 %copy-start.53 = (f32[32,1024]{1,0:T(8,128)S(1)}, f32[32,1024]{1,0:T(8,128)}, u32[]{:S(2)}) copy-start(f32[32,1024]{1,0:T(8,128)} %refs_1_.1) | copy-start | bytes 393220
  334.8 184.2 %copy-start.54 = (f32[2,32,1024]{2,1,0:T(8,128)S(1)}, f32[2,32,1024]{2,1,0:T(8,128)}, u32[]{:S(2)}) copy-start(f32[2,32,1024]{2,1,0:T(8,128)} %param.27) | copy-start | bytes 786436
  335.2 341.2 %copy-start.30 = (f32[32,3072]{1,0:T(8,128)S(1)}, f32[32,3072]{1,0:T(8,128)}, u32[]{:S(2)}) copy-start(f32[32,3072]{1,0:T(8,128)} %refs_2_.1) | copy-start | bytes 1179652
  335.2 341.2 %copy-start.49 = (f32[2,32,3072]{2,1,0:T(8,128)S(1)}, f32[2,32,3072]{2,1,0:T(8,128)}, u32[]{:S(2)}) copy-start(f32[2,32,3072]{2,1,0:T(8,128)} %param.26) | copy-start | bytes 2359300
  336.4 524.6 %copy-start.28 = (f32[32,4096]{1,0:T(8,128)S(1)}, f32[32,4096]{1,0:T(8,128)}, u32[]{:S(2)}) copy-start(f32[32,4096]{1,0:T(8,128)} %refs_3_.1) | copy-start | bytes 1572868
  336.4 524.6 %copy-start.35 = (f32[2,32,4096]{2,1,0:T(8,128)S(1)}, f32[2,32,4096]{2,1,0:T(8,128)}, u32[]{:S(2)}) copy-start(f32[2,32,4096]{2,1,0:T(8,128)} %param.28) | copy-start | bytes 3145732
  377.8 485.6 %copy-start.55 = (f32[8,32]{1,0:T(8,128)}, f32[8,32]{1,0:T(8,128)S(1)}, u32[]{:S(2)}) copy-start(f32[8,32]{1,0:T(8,128)S(1)} %copy.112) | copy-start | bytes 3076
  678.6 369.8 %copy-start.29 = (f32[128,1024]{1,0:T(8,128)S(1)}, f32[128,1024]{1,0:T(8,128)}, u32[]{:S(2)}) copy-start(f32[128,1024]{1,0:T(8,128)} %refs_4_.1) | copy-start | bytes 1572868
  678.6 369.8 %copy-start.36 = (f32[2,128,1024]{2,1,0:T(8,128)S(1)}, f32[2,128,1024]{2,1,0:T(8,128)}, u32[]{:S(2)}) copy-start(f32[2,128,1024]{2,1,0:T(8,128)} %param.29) | copy-start | bytes 3145732
  (37 other events, 83.0 us)
Sparse Core Ops, SparseCore 0:
  239.2 137.7 reduce-scatter.15
  379.8 139.1 reduce-scatter.9
  525.6 150.7 reduce-scatter.7
  679.1 181.8 reduce-scatter.11
  863.7 184.6 reduce-scatter.13

commit v2 on v1

--- a/solution.py
+++ b/solution.py
@@ -384,7 +384,718 @@
     return vec.transpose(1, 0, 2).reshape(8, -1).astype(jnp.bfloat16), bias.reshape(-1).astype(jnp.bfloat16)
 
 
-def body(
+F32, BF16 = jnp.float32, jnp.bfloat16
+
+
+def nn(a, b):
+    return lax.dot_general(a, b, (((1,), (0,)), ((), ())), preferred_element_type=F32)
+
+
+def nt(a, b):
+    return lax.dot_general(a, b, (((1,), (1,)), ((), ())), preferred_element_type=F32)
+
+
+def tn(a, b):
+    return lax.dot_general(a, b, (((0,), (0,)), ((), ())), preferred_element_type=F32)
+
+
+def chunks(total, size, work):
+    def step(i, carry):
+        work(pl.ds(pl.multiple_of(i * size, size), size))
+        return carry
+
+    lax.fori_loop(0, total // size, step, 0)
+
+
+def split_colours(columns, orders, shares):
+    found, at = [], 0
+    for order, share in zip(orders, shares):
+        if share:
+            found.append((at * 128, share * 128, order))
+            at += share
+    assert at * 128 == columns
+    return found
+
+
+class Spread:
+    def __init__(self, full, own, rows, columns, colours, place):
+        self.full, self.own, self.rows, self.columns, self.colours = full, own, rows, columns, colours
+        self.sizes, self.coords, self.core = place
+
+    def view(self, colour, fixed, core):
+        where = tuple(fixed.get(dim, slice(None)) for dim in range(3))
+        return self.full.at[(*where, core, pl.ds(*self.rows), pl.ds(self.columns + colour[0], colour[1]))]
+
+    def sends(self, stage):
+        for colour in self.colours:
+            order = colour[2]
+            dim = order[stage]
+            held = self.view(colour, {d: self.coords[d] for d in order[stage:]}, self.core)
+            source = held
+            if stage == 0:
+                source = self.own.at[pl.ds(*self.rows), pl.ds(self.columns + colour[0], colour[1])]
+            for step in range(1, self.sizes[dim]):
+                peer = swapped(self.coords, dim, (self.coords[dim] + step) % self.sizes[dim])
+                yield source, held, device_at(peer, self.core, self.sizes)
+
+    def passed(self, stage):
+        for colour in self.colours:
+            order = colour[2]
+            dim = order[stage]
+            fixed = {d: self.coords[d] for d in order[stage + 1:]}
+            if stage == 0:
+                yield self.view(colour, fixed, self.core)
+            else:
+                for step in range(1, self.sizes[dim]):
+                    yield self.view(colour, {**fixed, dim: (self.coords[dim] + step) % self.sizes[dim]}, self.core)
+
+
+class Group:
+    def __init__(self, sem, gauge):
+        self.sem, self.gauge, self.units = sem, gauge, 0
+
+    def count(self, ref):
+        self.units += math.prod(ref.shape) * jnp.dtype(ref.dtype).itemsize // 256
+
+    def wait(self):
+        whole = self.gauge.at[pl.ds(0, self.units)]
+        pltpu.make_async_copy(whole, whole, self.sem).wait()
+
+
+class Chunk:
+    def __init__(self, wires, parts):
+        self.wires, self.parts = wires, parts
+        self.arriving, self.swap = {}, wires.group()
+
+    def start(self, stage):
+        self.arriving[stage] = self.wires.group()
+        for part in self.parts:
+            for one in part.sends(stage):
+                self.wires.send(*one, self.arriving[stage])
+
+    def land(self, stage):
+        self.arriving[stage].wait()
+
+    def share(self, stage):
+        for part in self.parts:
+            for view in part.passed(stage):
+                self.wires.send(view, view, self.wires.partner, self.swap)
+
+    def finish(self):
+        self.swap.wait()
+
+
+class Wires:
+    def __init__(self, send_sem, recv_sem, gauge, partner):
+        self.recv_sem, self.gauge, self.partner = recv_sem, gauge, partner
+        self.used, self.sent = 0, Group(send_sem.at[0], gauge)
+
+    def group(self):
+        self.used += 1
+        return Group(self.recv_sem.at[self.used - 1], self.gauge)
+
+    def send(self, src, dst, target, group):
+        pltpu.make_async_remote_copy(
+            src_ref=src, dst_ref=dst, send_sem=self.sent.sem, recv_sem=group.sem,
+            device_id=(target,), device_id_type=MESH_ID,
+        ).start()
+        group.count(dst)
+        self.sent.count(dst)
+
+    def swap(self, src, dst):
+        group = self.group()
+        self.send(src, dst, self.partner, group)
+        return group
+
+    def drain(self):
+        self.sent.wait()
+
+
+class Reduce:
+    def __init__(self, wires, held, landing, colours, place):
+        self.wires, self.held, self.landing, self.colours = wires, held, landing, colours
+        self.sizes, self.coords, self.core = place
+
+    def view(self, colour, fixed):
+        where = tuple(fixed.get(dim, slice(None)) for dim in range(3))
+        return self.held.at[(*where, slice(None), pl.ds(colour[0], colour[1]))]
+
+    def start(self, stage):
+        self.arriving = self.wires.group()
+        for at, colour in enumerate(self.colours):
+            order = colour[2]
+            dim = order[stage]
+            fixed = {d: self.coords[d] for d in order[:stage]}
+            for step in range(1, self.sizes[dim]):
+                theirs = (self.coords[dim] + step) % self.sizes[dim]
+                peer = swapped(self.coords, dim, theirs)
+                self.wires.send(
+                    self.view(colour, {**fixed, dim: theirs}),
+                    self.landing[at][stage].at[step - 1],
+                    device_at(peer, self.core, self.sizes), self.arriving,
+                )
+
+    def land(self):
+        self.arriving.wait()
+
+    def add(self, stage, out=None):
+        rows = self.held.shape[3]
+        for at, colour in enumerate(self.colours):
+            order = colour[2]
+            fixed = {d: self.coords[d] for d in order[:stage + 1]}
+            free = [d for d in range(3) if d not in fixed]
+            landing = self.landing[at][stage]
+            counts = [self.sizes[d] for d in free]
+            total = math.prod(counts)
+            tall = min(rows, 32)
+
+            def step(i, carry, colour=colour, fixed=fixed, free=free, landing=landing, counts=counts, tall=tall):
+                where, rest, index = dict(fixed), i // (rows // tall), []
+                for d, size in zip(reversed(free), reversed(counts)):
+                    where[d] = rest % size
+                    index.insert(0, rest % size)
+                    rest = rest // size
+                span = pl.ds(pl.multiple_of((i % (rows // tall)) * tall, tall), tall)
+                place = (where[0], where[1], where[2], span, pl.ds(colour[0], colour[1]))
+                sums = self.held[place].astype(F32)
+                for other in range(landing.shape[0]):
+                    sums = sums + landing[(other, *index, span, slice(None))].astype(F32)
+                if out is None:
+                    self.held[place] = sums.astype(self.held.dtype)
+                else:
+                    out[span, pl.ds(colour[0], colour[1])] = sums
+                return carry
+
+            lax.fori_loop(0, total * (rows // tall), step, 0)
+
+
+def landing_shapes(rows, colours, sizes, dtype):
+    found = []
+    for _, width, order in colours:
+        stages = []
+        for stage in range(3):
+            free = [sizes[d] for d in range(3) if d not in order[:stage + 1]]
+            stages.append(pltpu.VMEM((sizes[order[stage]] - 1, *free, rows, width), dtype))
+        found.append(stages)
+    return found
+
+
+def stream(count, source, slots, sem, work):
+    def fetch(i, slot):
+        return pltpu.make_async_copy(source(i), slots(slot), sem.at[slot])
+
+    fetch(0, 0).start()
+
+    def step(i, carry):
+        slot = lax.rem(i, 2)
+
+        @pl.when(i + 1 < count)
+        def _():
+            fetch(i + 1, 1 - slot).start()
+
+        fetch(i, slot).wait()
+        work(i, slot)
+        return carry
+
+    lax.fori_loop(0, count, step, 0)
+
+
+def columns_of(i, width):
+    return pl.ds(pl.multiple_of(i * width, width), width)
+
+
+def row_stats(values):
+    mean = jnp.mean(values, axis=-1, keepdims=True)
+    centred = values - mean
+    rstd = lax.rsqrt(jnp.mean(centred * centred, axis=-1, keepdims=True) + ln_eps)
+    return centred * rstd, rstd
+
+
+SMALL, OUT, QKV, UP, DOWN = range(5)
+
+
+class Box(dict):
+    __getattr__ = dict.__getitem__
+
+
+def leaves(tree):
+    if isinstance(tree, dict):
+        tree = list(tree.values())
+    if isinstance(tree, list):
+        return [leaf for part in tree for leaf in leaves(part)]
+    return [] if tree is None else [tree]
+
+
+def shape_of(tree):
+    if isinstance(tree, dict):
+        return {name: shape_of(part) for name, part in tree.items()}
+    if isinstance(tree, list):
+        return [shape_of(part) for part in tree]
+    return tree is not None
+
+
+def unpack(shape, refs):
+    if isinstance(shape, dict):
+        return {name: unpack(part, refs) for name, part in shape.items()}
+    if isinstance(shape, list):
+        return [unpack(part, refs) for part in shape]
+    return next(refs) if shape else None
+
+
+GATHER_ORDERS = ((0, 1, 2), (0, 2, 1), (2, 1, 0))
+REDUCE_ORDERS = ((2, 1, 0), (1, 2, 0), (0, 1, 2))
+SHARES = {8: (3, 4, 1), 12: (5, 5, 2), 16: (7, 7, 2), 24: (11, 10, 3), 32: (14, 14, 4), 1: (1, 0, 0)}
+SIZES = (4, 2, 2)
+TILE = 512
+
+
+def step_kernel(names, *refs):
+    r = Box(unpack(names, iter(refs)))
+    sizes = SIZES
+    me = lax.axis_index("dp")
+    coords, core = locate(me, sizes)
+    place = (sizes, coords, core)
+    partner = device_at(coords, 1 - core, sizes)
+    rows, d = r.tokens.shape
+    ff = r.own[UP].shape[1]
+    heads2 = d // 128
+    slots = rows // MB_ROWS
+
+    for which in (OUT, QKV, UP, DOWN):
+        r.low[which][...] = r.own[which][...].astype(BF16)
+    r.low[SMALL] = r.own[SMALL]
+    greet(neighbours(coords, core, sizes))
+    wires = Wires(r.send_sem, r.recv_sem, r.gauge, partner)
+
+    def part(which, row_range, column_range):
+        start, width = column_range
+        colours = split_colours(width, GATHER_ORDERS, SHARES[width // 128])
+        return Spread(r.full[which], r.low[which], row_range, start, colours, place)
+
+    mine = []
+    for which in (SMALL, OUT, QKV, UP, DOWN):
+        copy = pltpu.make_async_copy(r.low[which], r.full[which].at[(*coords, core)], r.mine_sem.at[which])
+        copy.start()
+        mine.append(copy)
+    short, tall = r.own[OUT].shape[0], r.own[DOWN].shape[0]
+    parcels = [
+        Chunk(wires, [part(SMALL, (0, 16), (0, 128)), part(OUT, (0, short), (0, d))]),
+        Chunk(wires, [part(QKV, (0, short), (0, 3 * d // 2))]),
+        Chunk(wires, [part(QKV, (0, short), (3 * d // 2, 3 * d // 2))]),
+        Chunk(wires, [part(UP, (0, short), (0, ff // 2))]),
+        Chunk(wires, [part(UP, (0, short), (ff // 2, ff // 2))]),
+        Chunk(wires, [part(DOWN, (0, tall // 2), (0, d))]),
+        Chunk(wires, [part(DOWN, (tall // 2, tall // 2), (0, d))]),
+    ]
+    parcels[0].start(0)
+    dy_swap = wires.swap(r.dy, r.dy_far)
+
+    def norm_one(span):
+        normed, _ = row_stats(r.tokens[span, :].astype(F32))
+        r.da[span, :] = normed
+
+    chunks(rows, 32, norm_one)
+    for copy in mine:
+        copy.wait()
+    count = len(parcels)
+
+    def turn(t):
+        if t < count:
+            parcels[t].land(0)
+            if t + 1 < count:
+                parcels[t + 1].start(0)
+            parcels[t].start(1)
+            parcels[t].share(0)
+        if 0 <= t - 1 < count:
+            parcels[t - 1].land(1)
+            parcels[t - 1].start(2)
+            parcels[t - 1].share(1)
+        if 0 <= t - 2 < count:
+            parcels[t - 2].land(2)
+            parcels[t - 2].share(2)
+        if 0 <= t - 3 < count:
+            parcels[t - 3].finish()
+
+    for t in range(4):
+        turn(t)
+    copy = pltpu.make_async_copy(r.full[SMALL], r.smalls, r.mine_sem.at[0])
+    copy.start()
+    copy.wait()
+    devices = math.prod(sizes) * 2
+    flat = [(z, y, x, c) for z in range(sizes[0]) for y in range(sizes[1]) for x in range(sizes[2]) for c in range(2)]
+    per = devices * 128 // d
+    vec, bias = r.vec, r.bias
+    for j in range(d // 128):
+        total = 0.0
+        for k in range(per):
+            total = total + r.smalls[flat[j * per + k]].astype(F32)[0:8]
+        vec[:, j * 128:(j + 1) * 128] = total
+    for j in range(devices):
+        bias[:, j * 128:(j + 1) * 128] = r.smalls[flat[j]].astype(F32)[8:9]
+    for t in range(4, 6):
+        turn(t)
+
+    def first_in(span):
+        r.a[span, :] = (r.da[span, :] * vec[0:1, :] + vec[1:2, :]).astype(BF16)
+
+    chunks(rows, 32, first_in)
+
+    def transpose_out(source, turned, far):
+        width = source.shape[1]
+        block = turned.shape[2]
+        group = max(1, 256 // (2 * block))
+
+        def step(i, carry):
+            value = source[:, columns_of(i, 2 * block * group)]
+            flipped = value.astype(F32).T.astype(BF16)
+            turned[pl.ds(i * group, group)] = flipped.reshape(group, 2, block, rows)
+            return carry
+
+        lax.fori_loop(0, width // (2 * block * group), step, 0)
+        return wires.swap(turned.at[:, 1 - core], far)
+
+    def tile_stream(which, width, work):
+        full, slot = r.full[which], r.wide
+        total = full.shape[-1] // TILE
+        stream(
+            total,
+            lambda i: full.at[:, :, :, :, :, columns_of(i, TILE)],
+            lambda s: slot.at[s],
+            r.tile_sem,
+            lambda i, s: work(i, slot[s].reshape(-1, TILE)),
+        )
+
+    def qkv_tile(i, tile):
+        which = i * TILE // d
+        values = nn(r.a[...], tile)
+        shift = jnp.where(which == 0, 1.0, 0.0) * vec[2:3, columns_of(i % (d // TILE), TILE)] + jnp.where(
+            which == 2, 1.0, 0.0
+        ) * vec[3:4, columns_of(i % (d // TILE), TILE)]
+        r.qkv[:, columns_of(i, TILE)] = (values + shift).astype(BF16)
+
+    tile_stream(QKV, TILE, qkv_tile)
+    one_far = transpose_out(r.a, r.one_t, r.one_far)
+
+    low_lane = lax.broadcasted_iota(jnp.int32, (MB_ROWS, 128), 1) < HEAD_DIM
+    scale = 1.0 / math.sqrt(HEAD_DIM)
+
+    def stacked(value):
+        zero = jnp.zeros_like(value)
+        return jnp.concatenate([jnp.where(low_lane, value, zero), jnp.where(low_lane, zero, value)], axis=0)
+
+    def merged(value):
+        return jnp.where(low_lane, value[:MB_ROWS], value[MB_ROWS:])
+
+    def attend(p, carry):
+        row = lax.broadcasted_iota(jnp.int32, (2 * MB_ROWS, 128), 0)
+        dist = (row % MB_ROWS - lax.broadcasted_iota(jnp.int32, (2 * MB_ROWS, 128), 1)).astype(F32)
+        head = (2 * p + row // MB_ROWS).astype(F32)
+        alibi = jnp.where(dist >= 0, -jnp.exp2((head + 1.0) * (-8.0 / HEADS)) * dist, -1e30)
+        for s in range(slots):
+            span = pl.ds(s * MB_ROWS, MB_ROWS)
+            q = r.qkv[span, columns_of(p, 128)]
+            k = r.qkv[span, columns_of(p + heads2, 128)]
+            v = r.qkv[span, columns_of(p + 2 * heads2, 128)]
+            scores = nt(stacked(q), k) * scale + alibi
+            top = jnp.max(scores, axis=-1, keepdims=True)
+            grown = jnp.exp(scores - top)
+            probs = grown / jnp.sum(grown, axis=-1, keepdims=True)
+            r.probs[p * slots + s] = probs
+            r.attn[span, columns_of(p, 128)] = merged(nn(probs.astype(BF16), v)).astype(BF16)
+        return carry
+
+    lax.fori_loop(0, heads2, attend, 0)
+    attn_far = transpose_out(r.attn, r.attn_t, r.attn_far)
+
+    def out_tile(i, tile):
+        span = columns_of(i, TILE)
+        r.h1[:, span] = r.tokens[:, span].astype(F32) + nn(r.attn[...], tile) + vec[4:5, span]
+
+    tile_stream(OUT, TILE, out_tile)
+    turn(6)
+
+    def second_in(span):
+        normed, _ = row_stats(r.h1[span, :])
+        r.a[span, :] = (normed * vec[5:6, :] + vec[6:7, :]).astype(BF16)
+
+    chunks(rows, 32, second_in)
+    two_far = transpose_out(r.a, r.two_t, r.two_far)
+    turn(7)
+
+    def up_tile(i, tile):
+        pre = nn(r.a[...], tile) + bias[:, columns_of(i, TILE)]
+        value, slope = gelu_pair(pre)
+        r.act[:, columns_of(i, TILE)] = value.astype(BF16)
+        r.slope[:, columns_of(i, TILE)] = slope.astype(BF16)
+
+    tile_stream(UP, TILE, up_tile)
+    act_far = transpose_out(r.act, r.act_t, r.act_far)
+    dy_swap.wait()
+    turn(8)
+    act_far.wait()
+
+    reduces = [
+        Reduce(wires, held, landing, colours, place)
+        for held, landing, colours in zip(r.grad, r.landing, reduce_colours(d, ff))
+    ]
+
+    def weight_grad(which, turned, far, near_d, far_d, width):
+        grad = r.grad[which]
+        block = turned.shape[2]
+        total = near_d.shape[1] // width
+        groups = max(1, 16 * block // 512)
+        each = 16 // groups
+
+        def step(i, carry):
+            at, g = i // groups, i % groups
+            left = turned[pl.ds(g * each, each), core].reshape(each * block, rows)
+            other = far[pl.ds(g * each, each)].reshape(each * block, rows)
+            span = columns_of(at, width)
+            value = nn(left, near_d[:, span]) + nn(other, far_d[:, span])
+            value = value.astype(BF16)
+            if groups == 1:
+                grad[:, :, :, :, span] = value.reshape(*sizes, block, width)
+            else:
+                grad[g, :, :, :, span] = value.reshape(*sizes[1:], block, width)
+            return carry
+
+        assert groups in (1, sizes[0])
+        lax.fori_loop(0, total * groups, step, 0)
+
+    weight_grad(DOWN, r.act_t, r.act_far, r.dy, r.dy_far, 512)
+    reduces[DOWN].start(0)
+    turn(9)
+
+    sums = r.sums
+    sums[...] = jnp.zeros_like(sums)
+    acc = r.da
+
+    def begin(span):
+        acc[span, :] = r.h1[span, :] + vec[7:8, :]
+        sums[7:8, :] += jnp.sum(r.dy[span, :].astype(F32), axis=0, keepdims=True)
+
+    chunks(rows, 32, begin)
+
+    def down_tile(i, s):
+        tile = r.deep[s].reshape(-1, d)
+        wide = tile.shape[0]
+        span = columns_of(i, wide)
+        acc[...] += nn(r.act[:, span], tile)
+        d_pre = nt(r.dy[...], tile) * r.slope[:, span].astype(F32)
+        r.bias_sum[:, span] = jnp.sum(d_pre, axis=0, keepdims=True)
+        r.act[:, span] = d_pre.astype(BF16)
+
+    full_down = r.full[DOWN]
+    stream(
+        sizes[0] * sizes[1],
+        lambda i: full_down.at[i // sizes[1], i % sizes[1]],
+        lambda s: r.deep.at[s],
+        r.tile_sem,
+        down_tile,
+    )
+    pre_swap = wires.swap(r.act, r.pre_far)
+    r.output[...] = acc[...].astype(BF16)
+
+    def row_stream(which, left):
+        full, slot = r.full[which], r.flat
+        width = full.shape[-1]
+
+        def work(i, s):
+            tile = slot[s, :, :, :, :, pl.ds(0, width)].reshape(-1, width)
+            return nt(left[...], tile)
+
+        def run(put):
+            stream(
+                sizes[0],
+                lambda i: full.at[i],
+                lambda s: slot.at[s, :, :, :, :, pl.ds(0, width)],
+                r.tile_sem,
+                lambda i, s: put(i, work(i, s)),
+            )
+
+        return run
+
+    def put_da(i, value):
+        r.da[:, columns_of(i, value.shape[1])] = value
+
+    row_stream(UP, r.act)(put_da)
+    two_far.wait()
+    pre_swap.wait()
+    weight_grad(UP, r.two_t, r.two_far, r.act, r.pre_far, 512)
+    reduces[UP].start(0)
+
+    def norm_two_back(span):
+        normed, rstd = row_stats(r.h1[span, :])
+        da = r.da[span, :]
+        sums[5:6, :] += jnp.sum(da * normed, axis=0, keepdims=True)
+        sums[6:7, :] += jnp.sum(da, axis=0, keepdims=True)
+        d_h1 = r.dy[span, :].astype(F32) + norm_back(da, normed, rstd, vec[5:6, :])
+        sums[4:5, :] += jnp.sum(d_h1, axis=0, keepdims=True)
+        r.d_h1[span, :] = d_h1
+        r.d_mid[span, :] = d_h1.astype(BF16)
+
+    chunks(rows, 32, norm_two_back)
+    mid_swap = wires.swap(r.d_mid, r.mid_far)
+
+    def put_attn(i, value):
+        r.d_attn[:, columns_of(i, value.shape[1])] = value.astype(BF16)
+
+    row_stream(OUT, r.d_mid)(put_attn)
+
+    def advance(which, stage):
+        reduces[which].land()
+        reduces[which].add(stage - 1)
+        reduces[which].start(stage)
+
+    def complete(which):
+        reduces[which].land()
+        reduces[which].add(2, r.final[which])
+
+    advance(DOWN, 1)
+
+    def attend_back(p, carry):
+        span_p = columns_of(p, 128)
+        d_bq = jnp.zeros((1, 128), F32)
+        d_bv = jnp.zeros((1, 128), F32)
+        for s in range(slots):
+            span = pl.ds(s * MB_ROWS, MB_ROWS)
+            q = stacked(r.qkv[span, span_p])
+            k = r.qkv[span, columns_of(p + heads2, 128)]
+            v = r.qkv[span, columns_of(p + 2 * heads2, 128)]
+            do = r.d_attn[span, span_p]
+            probs = r.probs[p * slots + s]
+            both = stacked(do)
+            d_v = tn(probs.astype(BF16), both)
+            d_probs = nt(both, v)
+            weighed = do.astype(F32) * r.attn[span, span_p].astype(F32)
+            delta = jnp.sum(stacked(weighed), axis=-1, keepdims=True)
+            d_scores = (probs * (d_probs - delta)).astype(BF16)
+            d_q = merged(nn(d_scores, k)) * scale
+            d_k = tn(d_scores, q) * scale
+            d_bq += jnp.sum(d_q, axis=0, keepdims=True)
+            d_bv += jnp.sum(d_v, axis=0, keepdims=True)
+            r.qkv[span, span_p] = d_q.astype(BF16)
+            r.qkv[span, columns_of(p + heads2, 128)] = d_k.astype(BF16)
+            r.qkv[span, columns_of(p + 2 * heads2, 128)] = d_v.astype(BF16)
+        sums[2:3, span_p] = d_bq
+        sums[3:4, span_p] = d_bv
+        return carry
+
+    lax.fori_loop(0, heads2, attend_back, 0)
+    qkv_swap = wires.swap(r.qkv, r.qkv_far)
+    advance(DOWN, 2)
+    row_stream(QKV, r.qkv)(put_da)
+    one_far.wait()
+    qkv_swap.wait()
+    weight_grad(QKV, r.one_t, r.one_far, r.qkv, r.qkv_far, 512)
+    advance(UP, 1)
+    reduces[QKV].start(0)
+    attn_far.wait()
+    mid_swap.wait()
+    weight_grad(OUT, r.attn_t, r.attn_far, r.d_mid, r.mid_far, 512)
+    reduces[OUT].start(0)
+
+    def norm_one_back(span):
+        normed, rstd = row_stats(r.tokens[span, :].astype(F32))
+        da = r.da[span, :]
+        sums[0:1, :] += jnp.sum(da * normed, axis=0, keepdims=True)
+        sums[1:2, :] += jnp.sum(da, axis=0, keepdims=True)
+        r.input_grad[span, :] = r.d_h1[span, :] + norm_back(da, normed, rstd, vec[0:1, :])
+
+    chunks(rows, 32, norm_one_back)
+
+    bundle = r.bundle
+    for j in range(devices):
+        at = (j // per) * 128
+        bundle[flat[j]] = jnp.concatenate(
+            [sums[:, at:at + 128], jnp.broadcast_to(r.bias_sum[:, j * 128:(j + 1) * 128], (8, 128))], axis=0
+        )
+    tiny_swap = wires.swap(bundle.at[:, :, :, 1 - core], r.tiny_far)
+    complete(DOWN)
+    advance(UP, 2)
+    tiny_swap.wait()
+    r.grad[SMALL][...] = bundle[:, :, :, core] + r.tiny_far[...]
+    tiny = reduces[SMALL]
+    tiny.start(0)
+    advance(QKV, 1)
+    tiny.land()
+    tiny.add(0)
+    tiny.start(1)
+    complete(UP)
+    advance(OUT, 1)
+    tiny.land()
+    tiny.add(1)
+    tiny.start(2)
+    advance(QKV, 2)
+    tiny.land()
+    tiny.add(2, r.final[SMALL])
+    advance(OUT, 2)
+    complete(QKV)
+    complete(OUT)
+    wires.drain()
+
+
+def reduce_colours(d, ff):
+    return [[(0, 128, (2, 1, 0))]] + [
+        split_colours(width, REDUCE_ORDERS, SHARES[width // 128]) for width in (d, 3 * d, ff, d)
+    ]
+
+
+def fused_step(tokens, dy, small, w_qkv, w_out, w_up, w_down):
+    sizes = SIZES
+    rows, d = tokens.shape
+    ff = w_up.shape[1]
+    short, tall = w_out.shape[0], w_down.shape[0]
+    heads2 = d // 128
+    slots = rows // MB_ROWS
+    whole = lambda s: jax.ShapeDtypeStruct((*sizes, 2, *s), BF16)
+    like = jax.ShapeDtypeStruct
+    wide = ((16, 128), (short, d), (short, 3 * d), (short, ff), (tall, d))
+    v = pltpu.VMEM
+    turned, across = v((16, 2, short, rows), BF16), v((16, short, rows), BF16)
+    flat, double = v((rows, d), BF16), v((rows, d), F32)
+    inputs = dict(tokens=tokens, dy=dy, own=[small, w_out, w_qkv, w_up, w_down])
+    in_hbm = dict(full=[whole(s) for s in wide], gauge=like((180_224, 128), BF16))
+    in_vmem = dict(
+        output=like((rows, d), BF16), input_grad=like((rows, d), F32), final=[like(s, F32) for s in wide]
+    )
+    heights = (16, short, short, short, tall)
+    colours = reduce_colours(d, ff)
+    scratch = dict(
+        low=[None, *(v(s, BF16) for s in wide[1:])],
+        smalls=v((*sizes, 2, 16, 128), BF16), vec=v((8, d), F32), bias=v((1, ff), F32),
+        dy_far=flat, da=double, a=flat, qkv=v((rows, 3 * d), BF16), qkv_far=v((rows, 3 * d), BF16),
+        probs=v((heads2 * slots, 2 * MB_ROWS, 128), F32), attn=flat, h1=double,
+        act=v((rows, ff), BF16), slope=v((rows, ff), BF16), pre_far=v((rows, ff), BF16),
+        d_h1=double, d_mid=flat, mid_far=flat, d_attn=flat,
+        one_t=turned, one_far=across, attn_t=turned, attn_far=across, two_t=turned, two_far=across,
+        act_t=v((16, 2, tall, rows), BF16), act_far=v((16, tall, rows), BF16),
+        wide=v((2, *sizes, 2, short, TILE), BF16), deep=v((2, sizes[2], 2, tall, d), BF16),
+        flat=v((2, *sizes[1:], 2, short, ff), BF16),
+        grad=[v((*sizes, *s), BF16 if at else F32) for at, s in enumerate(wide)],
+        sums=v((8, d), F32), bias_sum=v((1, ff), F32),
+        bundle=v((*sizes, 2, 16, 128), F32), tiny_far=v((*sizes, 16, 128), F32),
+        landing=[landing_shapes(heights[at], colours[at], sizes, BF16 if at else F32) for at in range(5)],
+        send_sem=pltpu.SemaphoreType.DMA((1,)), recv_sem=pltpu.SemaphoreType.DMA((56,)),
+        mine_sem=pltpu.SemaphoreType.DMA((5,)), tile_sem=pltpu.SemaphoreType.DMA((2,)),
+    )
+    names = {**inputs, **in_hbm, **in_vmem, **scratch}
+    found = pl.pallas_call(
+        functools.partial(step_kernel, shape_of(names)),
+        out_shape=[*leaves(in_hbm), *leaves(in_vmem)],
+        in_specs=[pl.BlockSpec(memory_space=v)] * len(leaves(inputs)),
+        out_specs=[pl.BlockSpec(memory_space=pltpu.HBM)] * len(leaves(in_hbm))
+        + [pl.BlockSpec(memory_space=v)] * len(leaves(in_vmem)),
+        scratch_shapes=leaves(scratch),
+        compiler_params=pltpu.CompilerParams(
+            collective_id=1, has_side_effects=True, vmem_limit_bytes=67_000_000
+        ),
+        name="fused_step",
+    )(*leaves(inputs))
+    return Box(unpack(shape_of({**in_hbm, **in_vmem}), iter(found)))
+
+
+def general_body(
     tokens,
     cotangent,
     lengths,
@@ -478,6 +1189,35 @@
     )
 
 
+def body(
+    tokens, cotangent, lengths, vectors, bias_up, w_qkv, w_out, w_up, w_down,
+    mom_vectors, mom_bias_up, mom_qkv, mom_out, mom_up, mom_down,
+):
+    if grid_of(lax.axis_size("dp")) != SIZES:
+        return general_body(
+            tokens, cotangent, lengths, vectors, bias_up, w_qkv, w_out, w_up, w_down,
+            mom_vectors, mom_bias_up, mom_qkv, mom_out, mom_up, mom_down,
+        )
+    me = lax.axis_index("dp")
+    place = jnp.arange(tokens.shape[0]) % MB_ROWS
+    live = place < jnp.repeat(lengths, MB_ROWS)
+    dy = jnp.where(live[:, None], cotangent, jnp.zeros((), jnp.bfloat16))
+    small = small_block(vectors, bias_up, me).astype(jnp.bfloat16)
+    found = fused_step(tokens, dy, small, w_qkv, w_out, w_up, w_down)
+    width = vectors.shape[1]
+    g_vec = lax.dynamic_slice(found.final[SMALL], (0, (me % (128 // width)) * width), (8, width))
+    owned = (
+        g_vec, found.final[SMALL][8], found.final[QKV], found.final[OUT], found.final[UP], found.final[DOWN],
+    )
+    params = (vectors, bias_up, w_qkv, w_out, w_up, w_down)
+    moments = (mom_vectors, mom_bias_up, mom_qkv, mom_out, mom_up, mom_down)
+    news = [adamw(p, m, g, float(STEP)) for p, m, g in zip(params, moments, owned)]
+    return (
+        found.output, found.input_grad, *owned,
+        *(n[0] for n in news), *(n[1] for n in news), *(n[2] for n in news),
+    )
+
+
 def solution(mesh):
     in_specs = (
         P("dp", None),

time: 1070 us -> 283 us (0.26); the launches traced: 1060 us -> 282 us
  waiting for transfers between devices: 704 us -> 0 us
  Pallas kernels: 147 us -> 259 us
  matrix products: 109 us -> 0 us
  blocking collectives: 41.7 us -> 0 us
  between operations: 15.5 us -> 0.75 us
  local copies, waits for them, and re-layouts: 18.1 us -> 5.56 us
    reduce_scatter x4 -> x0, waiting for transfers between devices: 664 us -> none  [the longest x1 185 us: body(): lax.psum_scatter(summed[5], 'dp', scatter_dimension=0, tiled=True)]
    pallas_call x1, Pallas kernels: 147 us -> 259 us  [fused_step(): pl.pallas_call(functools.partial(step_kernel, shape_of(names)), out_shape...]
    dot_general x36 -> x0, matrix products: 109 us -> none  [the longest x24 94.7 us: product(): return jnp.dot(left, right, preferred_element_type=jnp.float32)]
    unnamed x1 -> x0, blocking collectives: 41.7 us -> none
    unnamed x6 -> x0, waiting for transfers between devices: 40.1 us -> none
  transfers between devices with their start and end apart: 5 -> 0, of which waited for: 5 -> 0; matrix products, arithmetic and copies ran while one was open for 6% -> 0% of each run, Pallas kernels for 0% -> 0%
where the time goes in v2:
time: 283 us; the launch traced here: 282 us
  Pallas kernels  259 us (92%)
  other arithmetic  16.9 us (6%)
  local copies, waits for them, and re-layouts  5.56 us (2%)
    pallas_call x1, Pallas kernels, fused_step(): pl.pallas_call(functools.partial(step_kernel, shape_of(names)), out_shape...  259 us
    add x6, other arithmetic, adamw(): first / corr_one / (jnp.sqrt(second / corr_two) + adam_eps)  13 us

profile of v2, /device:TPU:0, one launch (start us, length us, event | category | flops | bytes accessed | tf_op | source)
XLA Modules:
  0.0 282.4 jit_solution(15202881112315138151)
XLA Ops:
  0.7 0.7 fusion.7
  1.4 0.7 convert_bitcast_fusion
  2.1 0.8 dynamic_update_slice.7
  2.9 0.6 fusion.6.refs_2_
  3.5 1.9 broadcast_select_fusion.refs_1_
  5.4 259.2 %fused_step.1 = (bf16[4,2,2,2,16,128]{5,4,3,2,1,0:T(8,128)(2,1)}, bf16[4,2,2,2,32,1024]{5,4,3,2,1,0:T(8,128)(2,1)}, bf16[4,2,2,2,32,3072]{5,4,3,2,1,0:T(8,128)(2...) custom-call(bf16[256,1024]{1,0:T(8,128)(2,1)} %refs_0_.1, ...), custom_call_target="tpu_custom_call" | custom-call | tf_op jit(solution)/shard_map/fused_step/pallas_call | solution.py:1083
  264.6 0.0 copy-start.5
  264.6 0.0 copy-start.3
  264.6 0.0 copy-start.2
  264.6 0.0 copy-start.4
  264.6 0.0 copy-start.1
  264.6 0.0 copy-start
  264.7 1.4 multiply_add_fusion.5
  266.1 1.4 multiply_add_fusion.4
  267.5 1.9 multiply_add_fusion.3
  269.4 2.5 multiply_add_fusion.2
  271.9 2.9 %multiply_add_fusion = (f32[128,1024]{1,0:T(8,128)}, f32[128,1024]{1,0:T(8,128)}, f32[128,1024]{1,0:T(8,128)}) fusion(f32[128,1024]{1,0:T(8,128)} %refs_6_.1, f32[128,1024]{1,0:T(8,128)} %get-tuple-element.93, f32[2,128,1024]{2,1,0:T(8,128)} %param.29), kind=kLoop, calls=%fused_computation.7 | loop fusion | flops 1703936 | bytes 3670016 | tf_op jit(solution)/shard_map/add | solution.py:177
  274.8 2.9 %multiply_add_fusion.1 = (f32[32,4096]{1,0:T(8,128)}, f32[32,4096]{1,0:T(8,128)}, f32[32,4096]{1,0:T(8,128)}) fusion(f32[32,4096]{1,0:T(8,128)} %refs_5_.1, f32[32,4096]{1,0:T(8,128)} %get-tuple-element.92, f32[2,32,4096]{2,1,0:T(8,128)} %param.28), kind=kLoop, calls=%fused_computation.8 | loop fusion | flops 1703936 | bytes 3670016 | tf_op jit(solution)/shard_map/add | solution.py:177
  277.6 0.0 copy-done.5
  277.6 0.8 copy.48
  278.4 0.0 copy-done.3
  278.4 1.0 copy.49
  279.4 0.0 copy-done.2
  279.4 0.7 copy.50
  280.2 0.0 copy-done.4
  280.2 0.7 copy.51
  280.8 0.0 copy-done.1
  280.8 0.8 copy.52
  281.6 0.0 copy-done
  281.6 0.8 copy.53
  (1 shorter events, 0.0 us)
Async XLA Ops:
  264.6 13.0 %copy-start.5 = (bf16[256,1024]{1,0:T(8,128)(2,1)S(1)}, bf16[256,1024]{1,0:T(8,128)(2,1)}, u32[]{:S(2)}) copy-start(bf16[256,1024]{1,0:T(8,128)(2,1)} %get-tuple-element.86) | copy-start | bytes 1572868
  264.6 13.8 %copy-start.3 = (f32[256,1024]{1,0:T(8,128)S(1)}, f32[256,1024]{1,0:T(8,128)}, u32[]{:S(2)}) copy-start(f32[256,1024]{1,0:T(8,128)} %get-tuple-element.87) | copy-start | bytes 3145732
  264.6 14.8 %copy-start.2 = (f32[32,3072]{1,0:T(8,128)S(1)}, f32[32,3072]{1,0:T(8,128)}, u32[]{:S(2)}) copy-start(f32[32,3072]{1,0:T(8,128)} %get-tuple-element.90) | copy-start | bytes 1179652
  264.6 15.5 %copy-start.4 = (f32[32,1024]{1,0:T(8,128)S(1)}, f32[32,1024]{1,0:T(8,128)}, u32[]{:S(2)}) copy-start(f32[32,1024]{1,0:T(8,128)} %get-tuple-element.91) | copy-start | bytes 393220
  264.6 16.2 %copy-start.1 = (f32[32,4096]{1,0:T(8,128)S(1)}, f32[32,4096]{1,0:T(8,128)}, u32[]{:S(2)}) copy-start(f32[32,4096]{1,0:T(8,128)} %get-tuple-element.92) | copy-start | bytes 1572868
  264.6 17.0 %copy-start = (f32[128,1024]{1,0:T(8,128)S(1)}, f32[128,1024]{1,0:T(8,128)}, u32[]{:S(2)}) copy-start(f32[128,1024]{1,0:T(8,128)} %get-tuple-element.93) | copy-start | bytes 1572868

commit v3 on v2

--- a/solution.py
+++ b/solution.py
@@ -407,24 +407,30 @@
     lax.fori_loop(0, total // size, step, 0)
 
 
-def split_colours(columns, orders, shares):
-    found, at = [], 0
+def split_colours(start, shares, orders):
+    found = []
     for order, share in zip(orders, shares):
         if share:
-            found.append((at * 128, share * 128, order))
-            at += share
-    assert at * 128 == columns
+            found.append((start, share * 128, order))
+            start += share * 128
     return found
 
 
+def in_thirds(columns, last):
+    tiles = columns // 128
+    third = tiles * last // 8
+    first = (tiles - third) // 2
+    return first, tiles - third - first, third
+
+
 class Spread:
-    def __init__(self, full, own, rows, columns, colours, place):
-        self.full, self.own, self.rows, self.columns, self.colours = full, own, rows, columns, colours
+    def __init__(self, full, own, rows, colours, place):
+        self.full, self.own, self.rows, self.colours = full, own, rows, colours
         self.sizes, self.coords, self.core = place
 
     def view(self, colour, fixed, core):
         where = tuple(fixed.get(dim, slice(None)) for dim in range(3))
-        return self.full.at[(*where, core, pl.ds(*self.rows), pl.ds(self.columns + colour[0], colour[1]))]
+        return self.full.at[(*where, core, pl.ds(*self.rows), pl.ds(colour[0], colour[1]))]
 
     def sends(self, stage):
         for colour in self.colours:
@@ -433,7 +439,7 @@
             held = self.view(colour, {d: self.coords[d] for d in order[stage:]}, self.core)
             source = held
             if stage == 0:
-                source = self.own.at[pl.ds(*self.rows), pl.ds(self.columns + colour[0], colour[1])]
+                source = self.own.at[pl.ds(*self.rows), pl.ds(colour[0], colour[1])]
             for step in range(1, self.sizes[dim]):
                 peer = swapped(self.coords, dim, (self.coords[dim] + step) % self.sizes[dim])
                 yield source, held, device_at(peer, self.core, self.sizes)
@@ -492,6 +498,7 @@
 
     def group(self):
         self.used += 1
+        assert self.used <= self.recv_sem.shape[0]
         return Group(self.recv_sem.at[self.used - 1], self.gauge)
 
     def send(self, src, dst, target, group):
@@ -512,13 +519,13 @@
 
 
 class Reduce:
-    def __init__(self, wires, held, landing, colours, place):
-        self.wires, self.held, self.landing, self.colours = wires, held, landing, colours
+    def __init__(self, wires, held, rows, landing, colours, place):
+        self.wires, self.held, self.rows, self.landing, self.colours = wires, held, rows, landing, colours
         self.sizes, self.coords, self.core = place
 
     def view(self, colour, fixed):
         where = tuple(fixed.get(dim, slice(None)) for dim in range(3))
-        return self.held.at[(*where, slice(None), pl.ds(colour[0], colour[1]))]
+        return self.held.at[(*where, pl.ds(*self.rows), pl.ds(colour[0], colour[1]))]
 
     def start(self, stage):
         self.arriving = self.wires.group()
@@ -539,7 +546,7 @@
         self.arriving.wait()
 
     def add(self, stage, out=None):
-        rows = self.held.shape[3]
+        first, rows = self.rows
         for at, colour in enumerate(self.colours):
             order = colour[2]
             fixed = {d: self.coords[d] for d in order[:stage + 1]}
@@ -555,11 +562,13 @@
                     where[d] = rest % size
                     index.insert(0, rest % size)
                     rest = rest // size
-                span = pl.ds(pl.multiple_of((i % (rows // tall)) * tall, tall), tall)
+                low = (i % (rows // tall)) * tall
+                span = pl.ds(pl.multiple_of(first + low, tall), tall)
+                local = pl.ds(pl.multiple_of(low, tall), tall)
                 place = (where[0], where[1], where[2], span, pl.ds(colour[0], colour[1]))
                 sums = self.held[place].astype(F32)
                 for other in range(landing.shape[0]):
-                    sums = sums + landing[(other, *index, span, slice(None))].astype(F32)
+                    sums = sums + landing[(other, *index, local, slice(None))].astype(F32)
                 if out is None:
                     self.held[place] = sums.astype(self.held.dtype)
                 else:
@@ -644,7 +653,6 @@
 
 GATHER_ORDERS = ((0, 1, 2), (0, 2, 1), (2, 1, 0))
 REDUCE_ORDERS = ((2, 1, 0), (1, 2, 0), (0, 1, 2))
-SHARES = {8: (3, 4, 1), 12: (5, 5, 2), 16: (7, 7, 2), 24: (11, 10, 3), 32: (14, 14, 4), 1: (1, 0, 0)}
 SIZES = (4, 2, 2)
 TILE = 512
 
@@ -663,14 +671,21 @@
 
     for which in (OUT, QKV, UP, DOWN):
         r.low[which][...] = r.own[which][...].astype(BF16)
-    r.low[SMALL] = r.own[SMALL]
+    devices = math.prod(sizes) * 2
+    per = devices * 128 // d
+    block, narrow = r.block, 128 // per
+    block[...] = jnp.zeros_like(block)
+    for k in range(per):
+        here = jnp.where(me % per == k, 1.0, 0.0)
+        block[0:8, k * narrow:(k + 1) * narrow] = r.vectors[...] * here
+    block[8:9, :] = r.bias_up[...]
+    r.low[SMALL][...] = block[...].astype(BF16)
     greet(neighbours(coords, core, sizes))
     wires = Wires(r.send_sem, r.recv_sem, r.gauge, partner)
 
-    def part(which, row_range, column_range):
-        start, width = column_range
-        colours = split_colours(width, GATHER_ORDERS, SHARES[width // 128])
-        return Spread(r.full[which], r.low[which], row_range, start, colours, place)
+    def part(which, row_range, start, shares):
+        colours = split_colours(start, shares, GATHER_ORDERS)
+        return Spread(r.full[which], r.low[which], row_range, colours, place)
 
     mine = []
     for which in (SMALL, OUT, QKV, UP, DOWN):
@@ -678,16 +693,41 @@
         copy.start()
         mine.append(copy)
     short, tall = r.own[OUT].shape[0], r.own[DOWN].shape[0]
+    all_short = (0, short)
+    half, half_ff = 3 * d // 2, ff // 2
     parcels = [
-        Chunk(wires, [part(SMALL, (0, 16), (0, 128)), part(OUT, (0, short), (0, d))]),
-        Chunk(wires, [part(QKV, (0, short), (0, 3 * d // 2))]),
-        Chunk(wires, [part(QKV, (0, short), (3 * d // 2, 3 * d // 2))]),
-        Chunk(wires, [part(UP, (0, short), (0, ff // 2))]),
-        Chunk(wires, [part(UP, (0, short), (ff // 2, ff // 2))]),
-        Chunk(wires, [part(DOWN, (0, tall // 2), (0, d))]),
-        Chunk(wires, [part(DOWN, (tall // 2, tall // 2), (0, d))]),
+        Chunk(wires, [part(SMALL, (0, 16), 0, (1,)), part(OUT, all_short, 0, in_thirds(d, 0))]),
+        Chunk(wires, [part(QKV, all_short, 0, in_thirds(half, 0))]),
+        Chunk(wires, [part(QKV, all_short, half, in_thirds(half, 0))]),
+        Chunk(wires, [part(UP, all_short, 0, in_thirds(half_ff, 0))]),
+        Chunk(wires, [part(UP, all_short, half_ff, in_thirds(half_ff, 1))]),
+        Chunk(wires, [part(DOWN, (0, tall // 2), 0, in_thirds(d, 2))]),
+        Chunk(wires, [part(DOWN, (tall // 2, tall // 2), 0, in_thirds(d, 2))]),
     ]
-    parcels[0].start(0)
+
+    def begin_part(t):
+        parcels[t].start(0)
+
+    def first_axis(t):
+        parcels[t].land(0)
+        parcels[t].start(1)
+        parcels[t].share(0)
+
+    def second_axis(t):
+        parcels[t].land(1)
+        parcels[t].start(2)
+        parcels[t].share(1)
+
+    def third_axis(t):
+        parcels[t].land(2)
+        parcels[t].share(2)
+
+    begin_part(0)
+    begin_part(1)
+    for slot in range(slots):
+        span = pl.ds(slot * MB_ROWS, MB_ROWS)
+        live = lax.broadcasted_iota(jnp.int32, (MB_ROWS, d), 0) < r.lengths[slot]
+        r.dy[span, :] = jnp.where(live, r.cotangent[span, :].astype(F32), 0.0).astype(BF16)
     dy_swap = wires.swap(r.dy, r.dy_far)
 
     def norm_one(span):
@@ -697,33 +737,24 @@
     chunks(rows, 32, norm_one)
     for copy in mine:
         copy.wait()
-    count = len(parcels)
-
-    def turn(t):
-        if t < count:
-            parcels[t].land(0)
-            if t + 1 < count:
-                parcels[t + 1].start(0)
-            parcels[t].start(1)
-            parcels[t].share(0)
-        if 0 <= t - 1 < count:
-            parcels[t - 1].land(1)
-            parcels[t - 1].start(2)
-            parcels[t - 1].share(1)
-        if 0 <= t - 2 < count:
-            parcels[t - 2].land(2)
-            parcels[t - 2].share(2)
-        if 0 <= t - 3 < count:
-            parcels[t - 3].finish()
-
-    for t in range(4):
-        turn(t)
+    first_axis(0)
+    begin_part(2)
+    first_axis(1)
+    begin_part(3)
+    second_axis(0)
+    first_axis(2)
+    begin_part(4)
+    second_axis(1)
+    third_axis(0)
+    first_axis(3)
+    begin_part(5)
+    second_axis(2)
+    third_axis(1)
+    parcels[0].finish()
     copy = pltpu.make_async_copy(r.full[SMALL], r.smalls, r.mine_sem.at[0])
     copy.start()
     copy.wait()
-    devices = math.prod(sizes) * 2
     flat = [(z, y, x, c) for z in range(sizes[0]) for y in range(sizes[1]) for x in range(sizes[2]) for c in range(2)]
-    per = devices * 128 // d
     vec, bias = r.vec, r.bias
     for j in range(d // 128):
         total = 0.0
@@ -732,13 +763,19 @@
         vec[:, j * 128:(j + 1) * 128] = total
     for j in range(devices):
         bias[:, j * 128:(j + 1) * 128] = r.smalls[flat[j]].astype(F32)[8:9]
-    for t in range(4, 6):
-        turn(t)
 
     def first_in(span):
         r.a[span, :] = (r.da[span, :] * vec[0:1, :] + vec[1:2, :]).astype(BF16)
 
     chunks(rows, 32, first_in)
+    first_axis(4)
+    begin_part(6)
+    second_axis(3)
+    third_axis(2)
+    parcels[1].finish()
+    first_axis(5)
+    second_axis(4)
+    parcels[2].finish()
 
     def transpose_out(source, turned, far):
         width = source.shape[1]
@@ -754,15 +791,14 @@
         lax.fori_loop(0, width // (2 * block * group), step, 0)
         return wires.swap(turned.at[:, 1 - core], far)
 
-    def tile_stream(which, width, work):
+    def tile_stream(which, low, high, work):
         full, slot = r.full[which], r.wide
-        total = full.shape[-1] // TILE
         stream(
-            total,
-            lambda i: full.at[:, :, :, :, :, columns_of(i, TILE)],
+            (high - low) // TILE,
+            lambda i: full.at[:, :, :, :, :, columns_of(i + low // TILE, TILE)],
             lambda s: slot.at[s],
             r.tile_sem,
-            lambda i, s: work(i, slot[s].reshape(-1, TILE)),
+            lambda i, s: work(i + low // TILE, slot[s].reshape(-1, TILE)),
         )
 
     def qkv_tile(i, tile):
@@ -773,7 +809,7 @@
         ) * vec[3:4, columns_of(i % (d // TILE), TILE)]
         r.qkv[:, columns_of(i, TILE)] = (values + shift).astype(BF16)
 
-    tile_stream(QKV, TILE, qkv_tile)
+    tile_stream(QKV, 0, 3 * d, qkv_tile)
     one_far = transpose_out(r.a, r.one_t, r.one_far)
 
     low_lane = lax.broadcasted_iota(jnp.int32, (MB_ROWS, 128), 1) < HEAD_DIM
@@ -804,15 +840,19 @@
             r.attn[span, columns_of(p, 128)] = merged(nn(probs.astype(BF16), v)).astype(BF16)
         return carry
 
+    third_axis(3)
     lax.fori_loop(0, heads2, attend, 0)
+    first_axis(6)
+    second_axis(5)
     attn_far = transpose_out(r.attn, r.attn_t, r.attn_far)
 
     def out_tile(i, tile):
         span = columns_of(i, TILE)
         r.h1[:, span] = r.tokens[:, span].astype(F32) + nn(r.attn[...], tile) + vec[4:5, span]
 
-    tile_stream(OUT, TILE, out_tile)
-    turn(6)
+    tile_stream(OUT, 0, d, out_tile)
+    third_axis(4)
+    parcels[3].finish()
 
     def second_in(span):
         normed, _ = row_stats(r.h1[span, :])
@@ -820,7 +860,6 @@
 
     chunks(rows, 32, second_in)
     two_far = transpose_out(r.a, r.two_t, r.two_far)
-    turn(7)
 
     def up_tile(i, tile):
         pre = nn(r.a[...], tile) + bias[:, columns_of(i, TILE)]
@@ -828,21 +867,25 @@
         r.act[:, columns_of(i, TILE)] = value.astype(BF16)
         r.slope[:, columns_of(i, TILE)] = slope.astype(BF16)
 
-    tile_stream(UP, TILE, up_tile)
+    tile_stream(UP, 0, ff // 2, up_tile)
+    second_axis(6)
+    third_axis(5)
+    parcels[4].finish()
+    tile_stream(UP, ff // 2, ff, up_tile)
     act_far = transpose_out(r.act, r.act_t, r.act_far)
     dy_swap.wait()
-    turn(8)
     act_far.wait()
 
     reduces = [
-        Reduce(wires, held, landing, colours, place)
-        for held, landing, colours in zip(r.grad, r.landing, reduce_colours(d, ff))
+        Reduce(wires, r.grad[which], span, landing, colours, place)
+        for (which, span, colours), landing in zip(reduce_parts(short, tall, d, ff), r.landing)
     ]
 
-    def weight_grad(which, turned, far, near_d, far_d, width):
+    def weight_grad(which, turned, far, near_d, far_d, low, high):
         grad = r.grad[which]
         block = turned.shape[2]
-        total = near_d.shape[1] // width
+        width = 512
+        total = (high - low) // width
         groups = max(1, 16 * block // 512)
         each = 16 // groups
 
@@ -850,7 +893,7 @@
             at, g = i // groups, i % groups
             left = turned[pl.ds(g * each, each), core].reshape(each * block, rows)
             other = far[pl.ds(g * each, each)].reshape(each * block, rows)
-            span = columns_of(at, width)
+            span = columns_of(at + low // width, width)
             value = nn(left, near_d[:, span]) + nn(other, far_d[:, span])
             value = value.astype(BF16)
             if groups == 1:
@@ -862,9 +905,12 @@
         assert groups in (1, sizes[0])
         lax.fori_loop(0, total * groups, step, 0)
 
-    weight_grad(DOWN, r.act_t, r.act_far, r.dy, r.dy_far, 512)
-    reduces[DOWN].start(0)
-    turn(9)
+    weight_grad(DOWN, r.act_t, r.act_far, r.dy, r.dy_far, 0, d)
+    reduces[0].start(0)
+    reduces[1].start(0)
+    third_axis(6)
+    parcels[5].finish()
+    parcels[6].finish()
 
     sums = r.sums
     sums[...] = jnp.zeros_like(sums)
@@ -919,10 +965,24 @@
         r.da[:, columns_of(i, value.shape[1])] = value
 
     row_stream(UP, r.act)(put_da)
+
+    def advance(part, stage):
+        reduces[part].land()
+        reduces[part].add(stage - 1)
+        reduces[part].start(stage)
+
+    def complete(part, which):
+        reduces[part].land()
+        reduces[part].add(2, r.final[which])
+
+    advance(0, 1)
     two_far.wait()
     pre_swap.wait()
-    weight_grad(UP, r.two_t, r.two_far, r.act, r.pre_far, 512)
-    reduces[UP].start(0)
+    weight_grad(UP, r.two_t, r.two_far, r.act, r.pre_far, 0, ff // 2)
+    reduces[2].start(0)
+    advance(1, 1)
+    weight_grad(UP, r.two_t, r.two_far, r.act, r.pre_far, ff // 2, ff)
+    reduces[3].start(0)
 
     def norm_two_back(span):
         normed, rstd = row_stats(r.h1[span, :])
@@ -942,16 +1002,7 @@
 
     row_stream(OUT, r.d_mid)(put_attn)
 
-    def advance(which, stage):
-        reduces[which].land()
-        reduces[which].add(stage - 1)
-        reduces[which].start(stage)
-
-    def complete(which):
-        reduces[which].land()
-        reduces[which].add(2, r.final[which])
-
-    advance(DOWN, 1)
+    advance(0, 2)
 
     def attend_back(p, carry):
         span_p = columns_of(p, 128)
@@ -981,19 +1032,23 @@
         sums[3:4, span_p] = d_bv
         return carry
 
-    lax.fori_loop(0, heads2, attend_back, 0)
+    lax.fori_loop(0, heads2 // 2, attend_back, 0)
+    advance(1, 2)
+    lax.fori_loop(heads2 // 2, heads2, attend_back, 0)
     qkv_swap = wires.swap(r.qkv, r.qkv_far)
-    advance(DOWN, 2)
+    advance(2, 1)
     row_stream(QKV, r.qkv)(put_da)
     one_far.wait()
     qkv_swap.wait()
-    weight_grad(QKV, r.one_t, r.one_far, r.qkv, r.qkv_far, 512)
-    advance(UP, 1)
-    reduces[QKV].start(0)
+    weight_grad(QKV, r.one_t, r.one_far, r.qkv, r.qkv_far, 0, 3 * d // 2)
+    reduces[4].start(0)
+    advance(3, 1)
+    weight_grad(QKV, r.one_t, r.one_far, r.qkv, r.qkv_far, 3 * d // 2, 3 * d)
+    reduces[5].start(0)
     attn_far.wait()
     mid_swap.wait()
-    weight_grad(OUT, r.attn_t, r.attn_far, r.d_mid, r.mid_far, 512)
-    reduces[OUT].start(0)
+    weight_grad(OUT, r.attn_t, r.attn_far, r.d_mid, r.mid_far, 0, d)
+    reduces[6].start(0)
 
     def norm_one_back(span):
         normed, rstd = row_stats(r.tokens[span, :].astype(F32))
@@ -1011,37 +1066,50 @@
             [sums[:, at:at + 128], jnp.broadcast_to(r.bias_sum[:, j * 128:(j + 1) * 128], (8, 128))], axis=0
         )
     tiny_swap = wires.swap(bundle.at[:, :, :, 1 - core], r.tiny_far)
-    complete(DOWN)
-    advance(UP, 2)
+    tiny = reduces[7]
+    advance(2, 2)
+    complete(0, DOWN)
     tiny_swap.wait()
     r.grad[SMALL][...] = bundle[:, :, :, core] + r.tiny_far[...]
-    tiny = reduces[SMALL]
     tiny.start(0)
-    advance(QKV, 1)
-    tiny.land()
-    tiny.add(0)
-    tiny.start(1)
-    complete(UP)
-    advance(OUT, 1)
-    tiny.land()
-    tiny.add(1)
-    tiny.start(2)
-    advance(QKV, 2)
-    tiny.land()
-    tiny.add(2, r.final[SMALL])
-    advance(OUT, 2)
-    complete(QKV)
-    complete(OUT)
+    advance(4, 1)
+    advance(3, 2)
+    complete(1, DOWN)
+    advance(7, 1)
+    advance(5, 1)
+    advance(6, 1)
+    complete(2, UP)
+    advance(4, 2)
+    advance(7, 2)
+    complete(3, UP)
+    advance(5, 2)
+    advance(6, 2)
+    complete(7, SMALL)
+    complete(4, QKV)
+    complete(5, QKV)
+    complete(6, OUT)
     wires.drain()
 
 
-def reduce_colours(d, ff):
-    return [[(0, 128, (2, 1, 0))]] + [
-        split_colours(width, REDUCE_ORDERS, SHARES[width // 128]) for width in (d, 3 * d, ff, d)
+def reduce_parts(short, tall, d, ff):
+    rows, half, half_ff = (0, short), 3 * d // 2, ff // 2
+
+    def colours(start, width, last):
+        return split_colours(start, in_thirds(width, last), REDUCE_ORDERS)
+
+    return [
+        (DOWN, (0, tall // 2), colours(0, d, 2)),
+        (DOWN, (tall // 2, tall // 2), colours(0, d, 2)),
+        (UP, rows, colours(0, half_ff, 1)),
+        (UP, rows, colours(half_ff, half_ff, 1)),
+        (QKV, rows, colours(0, half, 0)),
+        (QKV, rows, colours(half, half, 0)),
+        (OUT, rows, colours(0, d, 0)),
+        (SMALL, (0, 16), [(0, 128, (2, 1, 0))]),
     ]
 
 
-def fused_step(tokens, dy, small, w_qkv, w_out, w_up, w_down):
+def fused_step(tokens, cotangent, lengths, vectors, bias_up, w_qkv, w_out, w_up, w_down):
     sizes = SIZES
     rows, d = tokens.shape
     ff = w_up.shape[1]
@@ -1054,15 +1122,16 @@
     v = pltpu.VMEM
     turned, across = v((16, 2, short, rows), BF16), v((16, short, rows), BF16)
     flat, double = v((rows, d), BF16), v((rows, d), F32)
-    inputs = dict(tokens=tokens, dy=dy, own=[small, w_out, w_qkv, w_up, w_down])
+    inputs = dict(
+        tokens=tokens, cotangent=cotangent, vectors=vectors, bias_up=bias_up, own=[None, w_out, w_qkv, w_up, w_down],
+    )
     in_hbm = dict(full=[whole(s) for s in wide], gauge=like((180_224, 128), BF16))
     in_vmem = dict(
         output=like((rows, d), BF16), input_grad=like((rows, d), F32), final=[like(s, F32) for s in wide]
     )
-    heights = (16, short, short, short, tall)
-    colours = reduce_colours(d, ff)
+    parts = reduce_parts(short, tall, d, ff)
     scratch = dict(
-        low=[None, *(v(s, BF16) for s in wide[1:])],
+        low=[v(s, BF16) for s in wide], block=v((16, 128), F32), dy=flat,
         smalls=v((*sizes, 2, 16, 128), BF16), vec=v((8, d), F32), bias=v((1, ff), F32),
         dy_far=flat, da=double, a=flat, qkv=v((rows, 3 * d), BF16), qkv_far=v((rows, 3 * d), BF16),
         probs=v((heads2 * slots, 2 * MB_ROWS, 128), F32), attn=flat, h1=double,
@@ -1075,15 +1144,18 @@
         grad=[v((*sizes, *s), BF16 if at else F32) for at, s in enumerate(wide)],
         sums=v((8, d), F32), bias_sum=v((1, ff), F32),
         bundle=v((*sizes, 2, 16, 128), F32), tiny_far=v((*sizes, 16, 128), F32),
-        landing=[landing_shapes(heights[at], colours[at], sizes, BF16 if at else F32) for at in range(5)],
-        send_sem=pltpu.SemaphoreType.DMA((1,)), recv_sem=pltpu.SemaphoreType.DMA((56,)),
+        landing=[
+            landing_shapes(span[1], colours, sizes, BF16 if which else F32) for which, span, colours in parts
+        ],
+        send_sem=pltpu.SemaphoreType.DMA((1,)), recv_sem=pltpu.SemaphoreType.DMA((61,)),
         mine_sem=pltpu.SemaphoreType.DMA((5,)), tile_sem=pltpu.SemaphoreType.DMA((2,)),
     )
-    names = {**inputs, **in_hbm, **in_vmem, **scratch}
+    names = {**dict(lengths=lengths), **inputs, **in_hbm, **in_vmem, **scratch}
     found = pl.pallas_call(
         functools.partial(step_kernel, shape_of(names)),
         out_shape=[*leaves(in_hbm), *leaves(in_vmem)],
-        in_specs=[pl.BlockSpec(memory_space=v)] * len(leaves(inputs)),
+        in_specs=[pl.BlockSpec(memory_space=pltpu.SMEM)]
+        + [pl.BlockSpec(memory_space=v)] * len(leaves(inputs)),
         out_specs=[pl.BlockSpec(memory_space=pltpu.HBM)] * len(leaves(in_hbm))
         + [pl.BlockSpec(memory_space=v)] * len(leaves(in_vmem)),
         scratch_shapes=leaves(scratch),
@@ -1091,8 +1163,84 @@
             collective_id=1, has_side_effects=True, vmem_limit_bytes=67_000_000
         ),
         name="fused_step",
+    )(lengths, *leaves(inputs))
+    return Box(unpack(shape_of({**in_hbm, **in_vmem}), iter(found)))
+
+
+def adam_kernel(shape, *refs):
+    r = Box(unpack(shape, iter(refs)))
+    me = lax.axis_index("dp")
+    count = float(STEP)
+
+    def put(at, param, first, second, grad):
+        update, new_first, new_second = adamw(param, (first, second), grad, count)
+        r.grads[at][...] = grad
+        r.updates[at][...] = update
+        r.firsts[at][...] = new_first
+        r.seconds[at][...] = new_second
+
+    for at in range(2, 6):
+        put(at, r.params[at][...], r.moments[at][0], r.moments[at][1], r.final[at - 1][...])
+    r.output[...] = r.early_output[...]
+    r.input_grad[...] = r.early_grad[...]
+
+    @pl.when(pl.program_id(0) == 0)
+    def _():
+        narrow = r.params[0].shape[1]
+        per = 128 // narrow
+        grad = jnp.zeros((8, narrow), F32)
+        for k in range(per):
+            grad = grad + jnp.where(me % per == k, 1.0, 0.0) * r.final[SMALL][0:8, k * narrow:(k + 1) * narrow]
+        put(0, r.params[0][...], r.moments[0][0], r.moments[0][1], grad)
+        put(1, r.params[1][...], r.moments[1][0:1], r.moments[1][1:2], r.final[SMALL][8:9, :])
+
+
+def adam(found, params, moments):
+    steps = 4
+
+    def whole(s):
+        return pl.BlockSpec(s, lambda i: (0,) * len(s))
+
+    def cut(s):
+        return pl.BlockSpec((*s[:-1], s[-1] // steps), lambda i: (0,) * (len(s) - 1) + (i,))
+
+    def tall(s):
+        return pl.BlockSpec((s[0] // steps, s[1]), lambda i: (i, 0))
+
+    def each(make):
+        return [make(p.shape) for p in params]
+
+    like = jax.ShapeDtypeStruct
+    outs = each(lambda s: like(s, F32))
+    specs = [whole(p.shape) if at < 2 else cut(p.shape) for at, p in enumerate(params)]
+    moment_specs = [whole(m.shape) if at < 2 else cut(m.shape) for at, m in enumerate(moments)]
+    inputs = dict(
+        params=list(params), moments=list(moments), final=found.final,
+        early_output=found.output, early_grad=found.input_grad,
+    )
+    input_specs = dict(
+        params=specs, moments=moment_specs, final=[whole((16, 128)), *specs[2:]],
+        early_output=tall(found.output.shape), early_grad=tall(found.input_grad.shape),
+    )
+    results = dict(
+        grads=outs, updates=outs, firsts=outs, seconds=outs,
+        output=like(found.output.shape, BF16), input_grad=like(found.input_grad.shape, F32),
+    )
+    result_specs = dict(
+        grads=specs, updates=specs, firsts=specs, seconds=specs,
+        output=tall(found.output.shape), input_grad=tall(found.input_grad.shape),
+    )
+    shape = shape_of({**inputs, **results})
+    done = pl.pallas_call(
+        functools.partial(adam_kernel, shape),
+        grid=(steps,),
+        out_shape=leaves(results),
+        in_specs=leaves(input_specs),
+        out_specs=leaves(result_specs),
+        compiler_params=pltpu.CompilerParams(vmem_limit_bytes=67_000_000),
+        name="adam",
     )(*leaves(inputs))
-    return Box(unpack(shape_of({**in_hbm, **in_vmem}), iter(found)))
+    return Box(unpack(shape_of(results), iter(done)))
 
 
 def general_body(
@@ -1198,23 +1346,20 @@
             tokens, cotangent, lengths, vectors, bias_up, w_qkv, w_out, w_up, w_down,
             mom_vectors, mom_bias_up, mom_qkv, mom_out, mom_up, mom_down,
         )
-    me = lax.axis_index("dp")
-    place = jnp.arange(tokens.shape[0]) % MB_ROWS
-    live = place < jnp.repeat(lengths, MB_ROWS)
-    dy = jnp.where(live[:, None], cotangent, jnp.zeros((), jnp.bfloat16))
-    small = small_block(vectors, bias_up, me).astype(jnp.bfloat16)
-    found = fused_step(tokens, dy, small, w_qkv, w_out, w_up, w_down)
-    width = vectors.shape[1]
-    g_vec = lax.dynamic_slice(found.final[SMALL], (0, (me % (128 // width)) * width), (8, width))
-    owned = (
-        g_vec, found.final[SMALL][8], found.final[QKV], found.final[OUT], found.final[UP], found.final[DOWN],
-    )
-    params = (vectors, bias_up, w_qkv, w_out, w_up, w_down)
-    moments = (mom_vectors, mom_bias_up, mom_qkv, mom_out, mom_up, mom_down)
-    news = [adamw(p, m, g, float(STEP)) for p, m, g in zip(params, moments, owned)]
+    span = bias_up.shape[0]
+    found = fused_step(tokens, cotangent, lengths, vectors, bias_up.reshape(1, span), w_qkv, w_out, w_up, w_down)
+    found.final[OUT], found.final[QKV] = found.final[QKV], found.final[OUT]
+    done = adam(
+        found,
+        (vectors, bias_up.reshape(1, span), w_qkv, w_out, w_up, w_down),
+        (mom_vectors, mom_bias_up, mom_qkv, mom_out, mom_up, mom_down),
+    )
+
+    def six(arrays):
+        return (arrays[0], arrays[1].reshape(span), *arrays[2:])
+
     return (
-        found.output, found.input_grad, *owned,
-        *(n[0] for n in news), *(n[1] for n in news), *(n[2] for n in news),
+        done.output, done.input_grad, *six(done.grads), *six(done.updates), *six(done.firsts), *six(done.seconds),
     )
 
 

time: 283 us -> 247 us (0.87)
  other arithmetic: 16.9 us -> 0 us
  Pallas kernels: 259 us -> 246 us
  local copies, waits for them, and re-layouts: 5.56 us -> 0 us
    pallas_call x1, Pallas kernels: 259 us -> 239 us  [fused_step(): pl.pallas_call(functools.partial(step_kernel, shape_of(names)), out_shape...]
    add x6 -> x0, other arithmetic: 13 us -> none  [adamw(): first / corr_one / (jnp.sqrt(second / corr_two) + adam_eps)]
    pallas_call x0 -> x1, Pallas kernels: none -> 7.44 us  [adam(): pl.pallas_call(functools.partial(adam_kernel, shape), grid=(steps,), out_...]
    unnamed x18 -> x0, local copies, waits for them, and re-layouts: 4.78 us -> none
where the time goes in v3:
time: 247 us
  Pallas kernels  246 us (100%)
    pallas_call x1, Pallas kernels, fused_step(): pl.pallas_call(functools.partial(step_kernel, shape_of(names)), out_shape...  239 us
    pallas_call x1, Pallas kernels, adam(): pl.pallas_call(functools.partial(adam_kernel, shape), grid=(steps,), out_...  7.44 us

profile of v3, /device:TPU:0, one launch (start us, length us, event | category | flops | bytes accessed | tf_op | source)
XLA Modules:
  0.0 246.7 jit_solution(3898169915969123441)
XLA Ops:
  0.7 238.6 %fused_step.1 = (bf16[4,2,2,2,16,128]{5,4,3,2,1,0:T(8,128)(2,1)}, bf16[4,2,2,2,32,1024]{5,4,3,2,1,0:T(8,128)(2,1)}, bf16[4,2,2,2,32,3072]{5,4,3,2,1,0:T(8,128)(2...) custom-call(s32[2]{0:T(128)} %refs_0_.2, ...), custom_call_target="tpu_custom_call" | custom-call | tf_op jit(solution)/shard_map/fused_step/pallas_call | solution.py:1154
  239.3 7.4 %adam.1 = (f32[8,32]{1,0:T(8,128)}, f32[1,128]{1,0:T(1,128)}, f32[32,3072]{1,0:T(8,128)}, f32[32,1024]{1,0:T(8,128)}, f32[32,4096]{1,0:T(8,128)}, /*index=5*/f32...) custom-call(f32[8,32]{1,0:T(8,128)} %refs_0_.3, ...), custom_call_target="tpu_custom_call" | custom-call | tf_op jit(solution)/shard_map/adam/pallas_call | solution.py:1234

commit v4 on v3

--- a/solution.py
+++ b/solution.py
@@ -424,36 +424,77 @@
 
 
 class Spread:
-    def __init__(self, full, own, rows, colours, place):
+    def __init__(self, full, own, rows, colours, relay, place):
         self.full, self.own, self.rows, self.colours = full, own, rows, colours
         self.sizes, self.coords, self.core = place
-
-    def view(self, colour, fixed, core):
+        self.hops = []
+        for colour in colours:
+            hops = []
+            for at, dim in enumerate(colour[2]):
+                fixed = {d: self.coords[d] for d in colour[2][at + 1:]}
+                hops += [(dim, kind, fixed) for kind in ((1, 2) if dim == 0 and relay else (0,))]
+            self.hops.append(hops)
+        self.count = len(self.hops[0])
+
+    def view(self, colour, fixed):
         where = tuple(fixed.get(dim, slice(None)) for dim in range(3))
-        return self.full.at[(*where, core, pl.ds(*self.rows), pl.ds(colour[0], colour[1]))]
-
-    def sends(self, stage):
-        for colour in self.colours:
-            order = colour[2]
-            dim = order[stage]
-            held = self.view(colour, {d: self.coords[d] for d in order[stage:]}, self.core)
-            source = held
-            if stage == 0:
-                source = self.own.at[pl.ds(*self.rows), pl.ds(colour[0], colour[1])]
-            for step in range(1, self.sizes[dim]):
-                peer = swapped(self.coords, dim, (self.coords[dim] + step) % self.sizes[dim])
-                yield source, held, device_at(peer, self.core, self.sizes)
-
-    def passed(self, stage):
-        for colour in self.colours:
-            order = colour[2]
-            dim = order[stage]
-            fixed = {d: self.coords[d] for d in order[stage + 1:]}
-            if stage == 0:
-                yield self.view(colour, fixed, self.core)
+        return self.full.at[(*where, self.core, pl.ds(*self.rows), pl.ds(colour[0], colour[1]))]
+
+    def peer(self, dim, value):
+        return device_at(swapped(self.coords, dim, value), self.core, self.sizes)
+
+    def mine(self, at, hop):
+        colour = self.colours[at]
+        dim, kind, fixed = self.hops[at][hop]
+        if kind == 2:
+            low = self.coords[0] // 2 * 2
+            return self.view(colour, {**fixed, 0: pl.ds(low, 2)})
+        return self.view(colour, {**fixed, dim: self.coords[dim]})
+
+    def far(self, at, hop):
+        colour = self.colours[at]
+        _, _, fixed = self.hops[at][hop]
+        return self.view(colour, {**fixed, 0: pl.ds(2 - self.coords[0] // 2 * 2, 2)})
+
+    def inner(self):
+        return (self.coords[0] + 1) // 2 == 1
+
+    def send(self, wires, hop, group):
+        for at, colour in enumerate(self.colours):
+            dim, kind, _ = self.hops[at][hop]
+            held = self.mine(at, hop)
+            source = held if hop else self.own.at[pl.ds(*self.rows), pl.ds(colour[0], colour[1])]
+            here = self.coords[dim]
+            if kind == 2:
+                group.count(held)
+                wires.send_if(self.inner(), source, held, self.peer(0, 3 - here), group)
+            elif kind == 1:
+                group.count(held)
+                wires.send(source, held, self.peer(0, here + 1 - 2 * (here % 2)), group)
             else:
                 for step in range(1, self.sizes[dim]):
-                    yield self.view(colour, {**fixed, dim: (self.coords[dim] + step) % self.sizes[dim]}, self.core)
+                    group.count(held)
+                    wires.send(source, held, self.peer(dim, (here + step) % self.sizes[dim]), group)
+
+    def pass_on(self, wires, hop, group):
+        here = self.coords[0]
+        for at in range(len(self.colours)):
+            if self.hops[at][hop][1] == 2:
+                far = self.far(at, hop)
+                wires.put(far, far, self.peer(0, here + 1 - 2 * (here % 2)), group, wires.sent_if)
+
+    def arrived(self, hop):
+        for at, colour in enumerate(self.colours):
+            dim, kind, fixed = self.hops[at][hop]
+            if hop == 0:
+                yield self.view(colour, {**fixed, **({0: pl.ds(self.coords[0] // 2 * 2, 2)} if kind == 1 else {})})
+            elif kind == 2:
+                yield self.far(at, hop)
+            elif kind == 1:
+                yield self.view(colour, {**fixed, 0: self.coords[0] + 1 - 2 * (self.coords[0] % 2)})
+            else:
+                for step in range(1, self.sizes[dim]):
+                    yield self.view(colour, {**fixed, dim: (self.coords[dim] + step) % self.sizes[dim]})
 
 
 class Group:
@@ -471,20 +512,35 @@
 class Chunk:
     def __init__(self, wires, parts):
         self.wires, self.parts = wires, parts
-        self.arriving, self.swap = {}, wires.group()
-
-    def start(self, stage):
-        self.arriving[stage] = self.wires.group()
+        self.arriving, self.swap, self.relayed = {}, wires.group(), set()
+        self.hops = parts[0].count
+
+    def start(self, hop):
+        self.arriving[hop] = self.wires.group()
         for part in self.parts:
-            for one in part.sends(stage):
-                self.wires.send(*one, self.arriving[stage])
-
-    def land(self, stage):
-        self.arriving[stage].wait()
-
-    def share(self, stage):
+            part.send(self.wires, hop, self.arriving[hop])
+
+    def relay(self, hop):
+        def forward():
+            self.arriving[hop].wait()
+            for part in self.parts:
+                part.pass_on(self.wires, hop, self.arriving[hop])
+
+        pl.when(self.parts[0].inner())(forward)
+        self.relayed.add(hop)
+
+    def land(self, hop):
+        if hop not in self.relayed and any(h[hop][1] == 2 for part in self.parts for h in part.hops):
+            self.relay(hop)
+        if hop in self.relayed:
+            pl.when(jnp.logical_not(self.parts[0].inner()))(self.arriving[hop].wait)
+        else:
+            self.arriving[hop].wait()
+        if hop + 1 < self.hops:
+            self.start(hop + 1)
         for part in self.parts:
-            for view in part.passed(stage):
+            for view in part.arrived(hop):
+                self.swap.count(view)
                 self.wires.send(view, view, self.wires.partner, self.swap)
 
     def finish(self):
@@ -494,28 +550,39 @@
 class Wires:
     def __init__(self, send_sem, recv_sem, gauge, partner):
         self.recv_sem, self.gauge, self.partner = recv_sem, gauge, partner
-        self.used, self.sent = 0, Group(send_sem.at[0], gauge)
+        self.used, self.sent, self.sent_if = 0, Group(send_sem.at[0], gauge), Group(send_sem.at[1], gauge)
+        self.condition = None
 
     def group(self):
         self.used += 1
         assert self.used <= self.recv_sem.shape[0]
         return Group(self.recv_sem.at[self.used - 1], self.gauge)
 
-    def send(self, src, dst, target, group):
+    def put(self, src, dst, target, group, sent=None):
         pltpu.make_async_remote_copy(
-            src_ref=src, dst_ref=dst, send_sem=self.sent.sem, recv_sem=group.sem,
+            src_ref=src, dst_ref=dst, send_sem=(sent or self.sent).sem, recv_sem=group.sem,
             device_id=(target,), device_id_type=MESH_ID,
         ).start()
-        group.count(dst)
-        self.sent.count(dst)
+        if sent is not None:
+            sent.count(dst)
+
+    def send(self, src, dst, target, group):
+        self.put(src, dst, target, group, self.sent)
+
+    def send_if(self, condition, src, dst, target, group):
+        self.condition = condition
+        pl.when(condition)(lambda: self.put(src, dst, target, group, self.sent_if))
 
     def swap(self, src, dst):
         group = self.group()
+        group.count(dst)
         self.send(src, dst, self.partner, group)
         return group
 
     def drain(self):
         self.sent.wait()
+        if self.condition is not None:
+            pl.when(self.condition)(self.sent_if.wait)
 
 
 class Reduce:
@@ -535,6 +602,7 @@
             fixed = {d: self.coords[d] for d in order[:stage]}
             for step in range(1, self.sizes[dim]):
                 theirs = (self.coords[dim] + step) % self.sizes[dim]
+                self.arriving.count(self.landing[at][stage].at[step - 1])
                 peer = swapped(self.coords, dim, theirs)
                 self.wires.send(
                     self.view(colour, {**fixed, dim: theirs}),
@@ -578,11 +646,104 @@
             lax.fori_loop(0, total * (rows // tall), step, 0)
 
 
-def landing_shapes(rows, colours, sizes, dtype):
+class LineReduce:
+    def __init__(self, wires, held, columns, landing, place, last):
+        self.wires, self.held, self.columns, self.landing = wires, held, columns, landing
+        self.sizes, (self.z, self.y, self.x), self.core = place
+        self.inner = (self.z + 1) // 2 == 1
+        self.own, self.beside = self.z // 2 * 2, self.z + 1 - 2 * (self.z % 2)
+        self.rest = (self.y, self.x) if last else (slice(None), slice(None))
+        self.spread = (self.y, self.x) if last else ((0, 2), (0, 2))
+        self.groups = [wires.group() for _ in landing]
+        for group, ref in zip(self.groups, landing):
+            group.count(ref)
+
+    def push(self, at, chip, *where):
+        source = self.held.at[(*where, slice(None), pl.ds(*self.columns))]
+        self.wires.put(source, self.landing[at], device_at(chip, self.core, self.sizes), self.groups[at])
+
+    def add(self, landing, *where, out=None):
+        counts = list(landing.shape[:-2])
+        rows, tall = landing.shape[-2], 32
+
+        def step(i, carry):
+            rest, index = i // (rows // tall), []
+            for size in reversed(counts):
+                index.insert(0, rest % size)
+                rest = rest // size
+            free, place = list(index), []
+            for entry in where:
+                if isinstance(entry, tuple):
+                    place.append(entry[0] + free.pop(0))
+                else:
+                    place.append(entry)
+            span = pl.ds(pl.multiple_of((i % (rows // tall)) * tall, tall), tall)
+            place = (*place, span, pl.ds(*self.columns))
+            sums = self.held[place].astype(F32) + landing[(*index, span, slice(None))].astype(F32)
+            if out is None:
+                self.held[place] = sums.astype(self.held.dtype)
+            else:
+                out[span, pl.ds(*self.columns)] = sums
+            return carry
+
+        lax.fori_loop(0, math.prod(counts) * (rows // tall), step, 0)
+
+    def start(self):
+        def outer():
+            chip = (self.beside, self.y, self.x)
+            self.push(0, chip, pl.ds(2 - self.own, 2), *self.rest)
+            self.push(2, chip, self.beside, *self.rest)
+
+        pl.when(jnp.logical_not(self.inner))(outer)
+        self.wires.sent.count(self.landing[0])
+        self.wires.sent.count(self.landing[2])
+
+    def across(self):
+        def middle():
+            self.groups[0].wait()
+            self.add(self.landing[0], (2 - self.own, 2), *self.spread)
+            self.push(1, (3 - self.z, self.y, self.x), pl.ds(2 - self.own, 2), *self.rest)
+
+        pl.when(self.inner)(middle)
+
+    def back(self):
+        def middle():
+            self.groups[1].wait()
+            self.add(self.landing[1], (self.own, 2), *self.spread)
+            self.push(2, (self.beside, self.y, self.x), self.beside, *self.rest)
+
+        pl.when(self.inner)(middle)
+
+    def complete(self, out):
+        self.groups[2].wait()
+        self.add(self.landing[2], self.z, *self.spread, out=out)
+
+    def second(self):
+        self.complete(None)
+        self.push(3, (self.z, 1 - self.y, self.x), self.z, 1 - self.y, slice(None))
+        self.wires.sent.count(self.landing[3])
+
+    def third(self):
+        self.groups[3].wait()
+        self.add(self.landing[3], self.z, self.y, (0, 2))
+        self.push(4, (self.z, self.y, 1 - self.x), self.z, self.y, 1 - self.x)
+        self.wires.sent.count(self.landing[4])
+
+    def finish(self, out):
+        self.groups[4].wait()
+        self.add(self.landing[4], self.z, self.y, self.x, out=out)
+
+
+def line_landing(rows, width, last):
+    leads = ((2,), (2,), ()) if last else ((2, 2, 2), (2, 2, 2), (2, 2), (2,), ())
+    return [pltpu.VMEM((*lead, rows, width), BF16) for lead in leads]
+
+
+def landing_shapes(rows, colours, sizes, dtype, count=3):
     found = []
     for _, width, order in colours:
         stages = []
-        for stage in range(3):
+        for stage in range(count):
             free = [sizes[d] for d in range(3) if d not in order[:stage + 1]]
             stages.append(pltpu.VMEM((sizes[order[stage]] - 1, *free, rows, width), dtype))
         found.append(stages)
@@ -654,6 +815,9 @@
 GATHER_ORDERS = ((0, 1, 2), (0, 2, 1), (2, 1, 0))
 REDUCE_ORDERS = ((2, 1, 0), (1, 2, 0), (0, 1, 2))
 SIZES = (4, 2, 2)
+EARLY_TILES = 4
+LATE_TILES = 4
+UP_EIGHTHS = (0, 0)
 TILE = 512
 
 
@@ -665,12 +829,22 @@
     place = (sizes, coords, core)
     partner = device_at(coords, 1 - core, sizes)
     rows, d = r.tokens.shape
-    ff = r.own[UP].shape[1]
+    ff = r.low[UP].shape[1]
     heads2 = d // 128
     slots = rows // MB_ROWS
 
-    for which in (OUT, QKV, UP, DOWN):
-        r.low[which][...] = r.own[which][...].astype(BF16)
+    others = neighbours(coords, core, sizes)
+    barrier = pltpu.get_barrier_semaphore()
+    for other in others:
+        pl.semaphore_signal(barrier, inc=1, device_id=(other,), device_id_type=MESH_ID)
+    loads = []
+    for at, (source, target) in enumerate(
+        [(r.own[which], r.fin[which]) for which in (OUT, QKV, UP, DOWN)]
+        + [(r.cotangent, r.dy), (r.tokens_in, r.tokens)]
+    ):
+        copy = pltpu.make_async_copy(source, target, r.load_sem.at[at])
+        copy.start()
+        loads.append(copy)
     devices = math.prod(sizes) * 2
     per = devices * 128 // d
     block, narrow = r.block, 128 // per
@@ -680,77 +854,76 @@
         block[0:8, k * narrow:(k + 1) * narrow] = r.vectors[...] * here
     block[8:9, :] = r.bias_up[...]
     r.low[SMALL][...] = block[...].astype(BF16)
-    greet(neighbours(coords, core, sizes))
+    for at, which in enumerate((OUT, QKV, UP, DOWN)):
+        loads[at].wait()
+        r.low[which][...] = r.fin[which][...].astype(BF16)
+    pl.semaphore_wait(barrier, len(others))
     wires = Wires(r.send_sem, r.recv_sem, r.gauge, partner)
 
-    def part(which, row_range, start, shares):
-        colours = split_colours(start, shares, GATHER_ORDERS)
-        return Spread(r.full[which], r.low[which], row_range, colours, place)
+    def part(which, row_range, start, shares, relay, orders=GATHER_ORDERS):
+        colours = split_colours(start, shares, orders)
+        return Spread(r.full[which], r.low[which], row_range, colours, relay, place)
 
     mine = []
     for which in (SMALL, OUT, QKV, UP, DOWN):
         copy = pltpu.make_async_copy(r.low[which], r.full[which].at[(*coords, core)], r.mine_sem.at[which])
         copy.start()
         mine.append(copy)
-    short, tall = r.own[OUT].shape[0], r.own[DOWN].shape[0]
+    short, tall = r.low[OUT].shape[0], r.low[DOWN].shape[0]
     all_short = (0, short)
-    half, half_ff = 3 * d // 2, ff // 2
-    parcels = [
-        Chunk(wires, [part(SMALL, (0, 16), 0, (1,)), part(OUT, all_short, 0, in_thirds(d, 0))]),
-        Chunk(wires, [part(QKV, all_short, 0, in_thirds(half, 0))]),
-        Chunk(wires, [part(QKV, all_short, half, in_thirds(half, 0))]),
-        Chunk(wires, [part(UP, all_short, 0, in_thirds(half_ff, 0))]),
-        Chunk(wires, [part(UP, all_short, half_ff, in_thirds(half_ff, 1))]),
-        Chunk(wires, [part(DOWN, (0, tall // 2), 0, in_thirds(d, 2))]),
-        Chunk(wires, [part(DOWN, (tall // 2, tall // 2), 0, in_thirds(d, 2))]),
-    ]
-
-    def begin_part(t):
-        parcels[t].start(0)
-
-    def first_axis(t):
-        parcels[t].land(0)
-        parcels[t].start(1)
-        parcels[t].share(0)
-
-    def second_axis(t):
-        parcels[t].land(1)
-        parcels[t].start(2)
-        parcels[t].share(1)
-
-    def third_axis(t):
-        parcels[t].land(2)
-        parcels[t].share(2)
-
-    begin_part(0)
-    begin_part(1)
+    half, half_ff, early = 3 * d // 2, ff // 2, EARLY_TILES * 128
+    rest = in_thirds(d - early, 0)
+    first = Chunk(wires, [part(SMALL, (0, 16), 0, (1,), False), part(OUT, all_short, 0, in_thirds(d, 0), False)])
+    qkv0 = Chunk(wires, [part(QKV, all_short, 0, in_thirds(half, 0), True)])
+    qkv1 = Chunk(wires, [part(QKV, all_short, half, in_thirds(half, 0), True)])
+    up0 = Chunk(wires, [part(UP, all_short, 0, in_thirds(half_ff, UP_EIGHTHS[0]), True)])
+    up1 = Chunk(wires, [part(UP, all_short, half_ff, in_thirds(half_ff, UP_EIGHTHS[1]), True)])
+    ahead = Chunk(wires, [part(DOWN, (0, tall), d - early, (EARLY_TILES,), True, GATHER_ORDERS[2:])])
+    down0 = Chunk(wires, [part(DOWN, (0, tall // 2), 0, rest, True)])
+    down1 = Chunk(wires, [part(DOWN, (tall // 2, tall // 2), 0, rest, True)])
+
+    first.start(0)
+    ahead.start(0)
+    qkv0.start(0)
+    qkv1.start(0)
+    loads[4].wait()
     for slot in range(slots):
         span = pl.ds(slot * MB_ROWS, MB_ROWS)
         live = lax.broadcasted_iota(jnp.int32, (MB_ROWS, d), 0) < r.lengths[slot]
-        r.dy[span, :] = jnp.where(live, r.cotangent[span, :].astype(F32), 0.0).astype(BF16)
+        r.dy[span, :] = jnp.where(live, r.dy[span, :].astype(F32), 0.0).astype(BF16)
     dy_swap = wires.swap(r.dy, r.dy_far)
 
     def norm_one(span):
         normed, _ = row_stats(r.tokens[span, :].astype(F32))
         r.da[span, :] = normed
 
+    loads[5].wait()
     chunks(rows, 32, norm_one)
     for copy in mine:
         copy.wait()
-    first_axis(0)
-    begin_part(2)
-    first_axis(1)
-    begin_part(3)
-    second_axis(0)
-    first_axis(2)
-    begin_part(4)
-    second_axis(1)
-    third_axis(0)
-    first_axis(3)
-    begin_part(5)
-    second_axis(2)
-    third_axis(1)
-    parcels[0].finish()
+    ahead.land(0)
+    first.land(0)
+    qkv0.land(0)
+    up0.start(0)
+    qkv1.land(0)
+    qkv0.relay(1)
+    first.land(1)
+    up0.land(0)
+    qkv0.land(1)
+    up1.start(0)
+    qkv1.relay(1)
+    first.land(2)
+    qkv1.land(1)
+    up0.relay(1)
+    qkv0.land(2)
+    ahead.land(1)
+    up1.land(0)
+    up0.land(1)
+    down0.start(0)
+    up1.relay(1)
+    qkv1.land(2)
+    first.finish()
+    qkv0.land(3)
     copy = pltpu.make_async_copy(r.full[SMALL], r.smalls, r.mine_sem.at[0])
     copy.start()
     copy.wait()
@@ -768,17 +941,20 @@
         r.a[span, :] = (r.da[span, :] * vec[0:1, :] + vec[1:2, :]).astype(BF16)
 
     chunks(rows, 32, first_in)
-    first_axis(4)
-    begin_part(6)
-    second_axis(3)
-    third_axis(2)
-    parcels[1].finish()
-    first_axis(5)
-    second_axis(4)
-    parcels[2].finish()
-
-    def transpose_out(source, turned, far):
-        width = source.shape[1]
+    down0.land(0)
+    up1.land(1)
+    up0.land(2)
+    down1.start(0)
+    ahead.land(2)
+    down0.relay(1)
+    qkv1.land(3)
+    qkv0.finish()
+    down1.land(0)
+    down0.land(1)
+    up1.land(2)
+    qkv1.finish()
+
+    def transpose_out(source, turned, far, low=0, high=16):
         block = turned.shape[2]
         group = max(1, 256 // (2 * block))
 
@@ -788,8 +964,9 @@
             turned[pl.ds(i * group, group)] = flipped.reshape(group, 2, block, rows)
             return carry
 
-        lax.fori_loop(0, width // (2 * block * group), step, 0)
-        return wires.swap(turned.at[:, 1 - core], far)
+        lax.fori_loop(low // group, high // group, step, 0)
+        span = pl.ds(low, high - low)
+        return wires.swap(turned.at[span, 1 - core], far.at[span])
 
     def tile_stream(which, low, high, work):
         full, slot = r.full[which], r.wide
@@ -840,10 +1017,13 @@
             r.attn[span, columns_of(p, 128)] = merged(nn(probs.astype(BF16), v)).astype(BF16)
         return carry
 
-    third_axis(3)
-    lax.fori_loop(0, heads2, attend, 0)
-    first_axis(6)
-    second_axis(5)
+    down1.relay(1)
+    up0.land(3)
+    lax.fori_loop(0, heads2 // 2, attend, 0)
+    down1.land(1)
+    down0.land(2)
+    ahead.relay(3)
+    lax.fori_loop(heads2 // 2, heads2, attend, 0)
     attn_far = transpose_out(r.attn, r.attn_t, r.attn_far)
 
     def out_tile(i, tile):
@@ -851,8 +1031,8 @@
         r.h1[:, span] = r.tokens[:, span].astype(F32) + nn(r.attn[...], tile) + vec[4:5, span]
 
     tile_stream(OUT, 0, d, out_tile)
-    third_axis(4)
-    parcels[3].finish()
+    up1.land(3)
+    up0.finish()
 
     def second_in(span):
         normed, _ = row_stats(r.h1[span, :])
@@ -860,6 +1040,7 @@
 
     chunks(rows, 32, second_in)
     two_far = transpose_out(r.a, r.two_t, r.two_far)
+    down1.land(2)
 
     def up_tile(i, tile):
         pre = nn(r.a[...], tile) + bias[:, columns_of(i, TILE)]
@@ -868,13 +1049,14 @@
         r.slope[:, columns_of(i, TILE)] = slope.astype(BF16)
 
     tile_stream(UP, 0, ff // 2, up_tile)
-    second_axis(6)
-    third_axis(5)
-    parcels[4].finish()
+    act_far0 = transpose_out(r.act, r.act_t, r.act_far, 0, 8)
+    down0.land(3)
+    up1.finish()
     tile_stream(UP, ff // 2, ff, up_tile)
-    act_far = transpose_out(r.act, r.act_t, r.act_far)
+    act_far1 = transpose_out(r.act, r.act_t, r.act_far, 8, 16)
     dy_swap.wait()
-    act_far.wait()
+    act_far0.wait()
+    act_far1.wait()
 
     reduces = [
         Reduce(wires, r.grad[which], span, landing, colours, place)
@@ -884,7 +1066,7 @@
     def weight_grad(which, turned, far, near_d, far_d, low, high):
         grad = r.grad[which]
         block = turned.shape[2]
-        width = 512
+        width = 512 if (high - low) % 512 == 0 and low % 512 == 0 else high - low
         total = (high - low) // width
         groups = max(1, 16 * block // 512)
         each = 16 // groups
@@ -893,7 +1075,7 @@
             at, g = i // groups, i % groups
             left = turned[pl.ds(g * each, each), core].reshape(each * block, rows)
             other = far[pl.ds(g * each, each)].reshape(each * block, rows)
-            span = columns_of(at + low // width, width)
+            span = pl.ds(pl.multiple_of(low + at * width, 128), width)
             value = nn(left, near_d[:, span]) + nn(other, far_d[:, span])
             value = value.astype(BF16)
             if groups == 1:
@@ -905,12 +1087,18 @@
         assert groups in (1, sizes[0])
         lax.fori_loop(0, total * groups, step, 0)
 
-    weight_grad(DOWN, r.act_t, r.act_far, r.dy, r.dy_far, 0, d)
+    late = LATE_TILES * 128
+    weight_grad(DOWN, r.act_t, r.act_far, r.dy, r.dy_far, d - late, d)
+    line = LineReduce(wires, r.grad[DOWN], (d - late, late), r.line[0], place, False)
+    line.start()
+    weight_grad(DOWN, r.act_t, r.act_far, r.dy, r.dy_far, 0, d - late)
     reduces[0].start(0)
     reduces[1].start(0)
-    third_axis(6)
-    parcels[5].finish()
-    parcels[6].finish()
+    ahead.land(3)
+    down1.land(3)
+    down0.finish()
+    down1.finish()
+    ahead.finish()
 
     sums = r.sums
     sums[...] = jnp.zeros_like(sums)
@@ -932,15 +1120,49 @@
         r.act[:, span] = d_pre.astype(BF16)
 
     full_down = r.full[DOWN]
-    stream(
-        sizes[0] * sizes[1],
-        lambda i: full_down.at[i // sizes[1], i % sizes[1]],
-        lambda s: r.deep.at[s],
-        r.tile_sem,
-        down_tile,
-    )
-    pre_swap = wires.swap(r.act, r.pre_far)
-    r.output[...] = acc[...].astype(BF16)
+    tiles = sizes[0] * sizes[1]
+
+    def down_pass(low):
+        stream(
+            tiles // 2,
+            lambda i: full_down.at[(i + low) // sizes[1], (i + low) % sizes[1]],
+            lambda s: r.deep.at[s],
+            r.tile_sem,
+            lambda i, s: down_tile(i + low, s),
+        )
+        span = pl.ds(low * (ff // tiles), ff // 2)
+        return wires.swap(r.act.at[:, span], r.pre_far.at[:, span])
+
+    def advance(part, stage):
+        reduces[part].land()
+        reduces[part].add(stage - 1)
+        reduces[part].start(stage)
+
+    def complete(part, which):
+        reduces[part].land()
+        reduces[part].add(2, r.fin[which])
+
+    down_line = LineReduce(wires, r.grad[DOWN], (0, d - late), r.line[1], place, True)
+    up_lines = [
+        LineReduce(wires, r.grad[UP], (at * ff // 2, ff // 2), r.line[2 + at], place, True) for at in range(2)
+    ]
+
+    def settle(part):
+        reduces[part].land()
+        reduces[part].add(1)
+
+    pre_swap0 = down_pass(0)
+    advance(0, 1)
+    pre_swap1 = down_pass(tiles // 2)
+    advance(1, 1)
+    two_far.wait()
+    pre_swap0.wait()
+    weight_grad(UP, r.two_t, r.two_far, r.act, r.pre_far, 0, ff // 2)
+    reduces[2].start(0)
+    pre_swap1.wait()
+    weight_grad(UP, r.two_t, r.two_far, r.act, r.pre_far, ff // 2, ff)
+    reduces[3].start(0)
+    r.a[...] = acc[...].astype(BF16)
 
     def row_stream(which, left):
         full, slot = r.full[which], r.flat
@@ -966,23 +1188,7 @@
 
     row_stream(UP, r.act)(put_da)
 
-    def advance(part, stage):
-        reduces[part].land()
-        reduces[part].add(stage - 1)
-        reduces[part].start(stage)
-
-    def complete(part, which):
-        reduces[part].land()
-        reduces[part].add(2, r.final[which])
-
-    advance(0, 1)
-    two_far.wait()
-    pre_swap.wait()
-    weight_grad(UP, r.two_t, r.two_far, r.act, r.pre_far, 0, ff // 2)
-    reduces[2].start(0)
-    advance(1, 1)
-    weight_grad(UP, r.two_t, r.two_far, r.act, r.pre_far, ff // 2, ff)
-    reduces[3].start(0)
+    line.across()
 
     def norm_two_back(span):
         normed, rstd = row_stats(r.h1[span, :])
@@ -991,10 +1197,18 @@
         sums[6:7, :] += jnp.sum(da, axis=0, keepdims=True)
         d_h1 = r.dy[span, :].astype(F32) + norm_back(da, normed, rstd, vec[5:6, :])
         sums[4:5, :] += jnp.sum(d_h1, axis=0, keepdims=True)
-        r.d_h1[span, :] = d_h1
+        r.h1[span, :] = d_h1
         r.d_mid[span, :] = d_h1.astype(BF16)
 
     chunks(rows, 32, norm_two_back)
+    stores = []
+
+    def keep(source, target):
+        copy = pltpu.make_async_copy(source, target, r.store_sem.at[len(stores)])
+        copy.start()
+        stores.append(copy)
+
+    keep(r.a, r.output)
     mid_swap = wires.swap(r.d_mid, r.mid_far)
 
     def put_attn(i, value):
@@ -1002,7 +1216,13 @@
 
     row_stream(OUT, r.d_mid)(put_attn)
 
-    advance(0, 2)
+    advance(2, 1)
+    settle(0)
+    settle(1)
+    down_line.start()
+    attn_far.wait()
+    mid_swap.wait()
+    weight_grad(OUT, r.attn_t, r.attn_far, r.d_mid, r.mid_far, 0, d)
 
     def attend_back(p, carry):
         span_p = columns_of(p, 128)
@@ -1033,31 +1253,34 @@
         return carry
 
     lax.fori_loop(0, heads2 // 2, attend_back, 0)
-    advance(1, 2)
+    advance(3, 1)
+    reduces[4].start(0)
     lax.fori_loop(heads2 // 2, heads2, attend_back, 0)
     qkv_swap = wires.swap(r.qkv, r.qkv_far)
-    advance(2, 1)
+    down_line.across()
     row_stream(QKV, r.qkv)(put_da)
+    settle(2)
+    up_lines[0].start()
     one_far.wait()
     qkv_swap.wait()
-    weight_grad(QKV, r.one_t, r.one_far, r.qkv, r.qkv_far, 0, 3 * d // 2)
-    reduces[4].start(0)
-    advance(3, 1)
-    weight_grad(QKV, r.one_t, r.one_far, r.qkv, r.qkv_far, 3 * d // 2, 3 * d)
+    weight_grad(QKV, r.one_t, r.one_far, r.qkv, r.qkv_far, 0, d)
     reduces[5].start(0)
-    attn_far.wait()
-    mid_swap.wait()
-    weight_grad(OUT, r.attn_t, r.attn_far, r.d_mid, r.mid_far, 0, d)
+    weight_grad(QKV, r.one_t, r.one_far, r.qkv, r.qkv_far, d, 2 * d)
     reduces[6].start(0)
+    settle(3)
+    up_lines[1].start()
+    weight_grad(QKV, r.one_t, r.one_far, r.qkv, r.qkv_far, 2 * d, 3 * d)
+    line.back()
 
     def norm_one_back(span):
         normed, rstd = row_stats(r.tokens[span, :].astype(F32))
         da = r.da[span, :]
         sums[0:1, :] += jnp.sum(da * normed, axis=0, keepdims=True)
         sums[1:2, :] += jnp.sum(da, axis=0, keepdims=True)
-        r.input_grad[span, :] = r.d_h1[span, :] + norm_back(da, normed, rstd, vec[0:1, :])
+        r.h1[span, :] = r.h1[span, :] + norm_back(da, normed, rstd, vec[0:1, :])
 
     chunks(rows, 32, norm_one_back)
+    down_line.back()
 
     bundle = r.bundle
     for j in range(devices):
@@ -1066,45 +1289,62 @@
             [sums[:, at:at + 128], jnp.broadcast_to(r.bias_sum[:, j * 128:(j + 1) * 128], (8, 128))], axis=0
         )
     tiny_swap = wires.swap(bundle.at[:, :, :, 1 - core], r.tiny_far)
-    tiny = reduces[7]
-    advance(2, 2)
-    complete(0, DOWN)
+    tiny = reduces[8]
+    keep(r.h1, r.input_grad)
+    advance(4, 1)
+    up_lines[0].across()
     tiny_swap.wait()
     r.grad[SMALL][...] = bundle[:, :, :, core] + r.tiny_far[...]
     tiny.start(0)
-    advance(4, 1)
-    advance(3, 2)
-    complete(1, DOWN)
+    advance(5, 1)
+    reduces[7].start(0)
+    up_lines[1].across()
+    line.second()
+    down_line.complete(r.fin[DOWN])
+    advance(6, 1)
+    up_lines[0].back()
+    advance(4, 2)
+    advance(5, 2)
+    up_lines[1].back()
     advance(7, 1)
-    advance(5, 1)
-    advance(6, 1)
-    complete(2, UP)
-    advance(4, 2)
+    advance(6, 2)
+    line.third()
+    up_lines[0].complete(r.fin[UP])
     advance(7, 2)
-    complete(3, UP)
-    advance(5, 2)
-    advance(6, 2)
-    complete(7, SMALL)
-    complete(4, QKV)
+    advance(8, 1)
+    line.finish(r.fin[DOWN])
+    keep(r.fin[DOWN], r.final[DOWN])
+    advance(8, 2)
+    up_lines[1].complete(r.fin[UP])
+    complete(4, OUT)
+    keep(r.fin[UP], r.final[UP])
     complete(5, QKV)
-    complete(6, OUT)
+    keep(r.fin[OUT], r.final[OUT])
+    complete(6, QKV)
+    complete(8, SMALL)
+    keep(r.fin[SMALL], r.final[SMALL])
+    complete(7, QKV)
+    keep(r.fin[QKV], r.final[QKV])
+    for copy in stores:
+        copy.wait()
     wires.drain()
 
 
 def reduce_parts(short, tall, d, ff):
-    rows, half, half_ff = (0, short), 3 * d // 2, ff // 2
+    rows, half_ff = (0, short), ff // 2
 
     def colours(start, width, last):
         return split_colours(start, in_thirds(width, last), REDUCE_ORDERS)
 
     return [
-        (DOWN, (0, tall // 2), colours(0, d, 2)),
-        (DOWN, (tall // 2, tall // 2), colours(0, d, 2)),
-        (UP, rows, colours(0, half_ff, 1)),
-        (UP, rows, colours(half_ff, half_ff, 1)),
-        (QKV, rows, colours(0, half, 0)),
-        (QKV, rows, colours(half, half, 0)),
+        (DOWN, (0, tall // 2), colours(0, d - LATE_TILES * 128, 0)),
+        (DOWN, (tall // 2, tall // 2), colours(0, d - LATE_TILES * 128, 0)),
+        (UP, rows, colours(0, half_ff, 0)),
+        (UP, rows, colours(half_ff, half_ff, 0)),
         (OUT, rows, colours(0, d, 0)),
+        (QKV, rows, colours(0, d, 0)),
+        (QKV, rows, colours(d, d, 0)),
+        (QKV, rows, colours(2 * d, d, 0)),
         (SMALL, (0, 16), [(0, 128, (2, 1, 0))]),
     ]
 
@@ -1122,21 +1362,21 @@
     v = pltpu.VMEM
     turned, across = v((16, 2, short, rows), BF16), v((16, short, rows), BF16)
     flat, double = v((rows, d), BF16), v((rows, d), F32)
-    inputs = dict(
-        tokens=tokens, cotangent=cotangent, vectors=vectors, bias_up=bias_up, own=[None, w_out, w_qkv, w_up, w_down],
-    )
-    in_hbm = dict(full=[whole(s) for s in wide], gauge=like((180_224, 128), BF16))
-    in_vmem = dict(
-        output=like((rows, d), BF16), input_grad=like((rows, d), F32), final=[like(s, F32) for s in wide]
+    near = dict(vectors=vectors, bias_up=bias_up)
+    distant = dict(tokens_in=tokens, cotangent=cotangent, own=[None, w_out, w_qkv, w_up, w_down])
+    results = dict(
+        full=[whole(s) for s in wide], gauge=like((180_224, 128), BF16),
+        output=like((rows, d), BF16), input_grad=like((rows, d), F32), final=[like(s, F32) for s in wide],
     )
     parts = reduce_parts(short, tall, d, ff)
     scratch = dict(
-        low=[v(s, BF16) for s in wide], block=v((16, 128), F32), dy=flat,
+        low=[v(s, BF16) for s in wide], block=v((16, 128), F32), dy=flat, tokens=flat,
+        fin=[v(s, F32) for s in wide],
         smalls=v((*sizes, 2, 16, 128), BF16), vec=v((8, d), F32), bias=v((1, ff), F32),
         dy_far=flat, da=double, a=flat, qkv=v((rows, 3 * d), BF16), qkv_far=v((rows, 3 * d), BF16),
         probs=v((heads2 * slots, 2 * MB_ROWS, 128), F32), attn=flat, h1=double,
         act=v((rows, ff), BF16), slope=v((rows, ff), BF16), pre_far=v((rows, ff), BF16),
-        d_h1=double, d_mid=flat, mid_far=flat, d_attn=flat,
+        d_mid=flat, mid_far=flat, d_attn=flat,
         one_t=turned, one_far=across, attn_t=turned, attn_far=across, two_t=turned, two_far=across,
         act_t=v((16, 2, tall, rows), BF16), act_far=v((16, tall, rows), BF16),
         wide=v((2, *sizes, 2, short, TILE), BF16), deep=v((2, sizes[2], 2, tall, d), BF16),
@@ -1145,26 +1385,32 @@
         sums=v((8, d), F32), bias_sum=v((1, ff), F32),
         bundle=v((*sizes, 2, 16, 128), F32), tiny_far=v((*sizes, 16, 128), F32),
         landing=[
-            landing_shapes(span[1], colours, sizes, BF16 if which else F32) for which, span, colours in parts
+            landing_shapes(span[1], colours, sizes, BF16 if which else F32, 2 if which in (UP, DOWN) else 3)
+            for which, span, colours in parts
         ],
-        send_sem=pltpu.SemaphoreType.DMA((1,)), recv_sem=pltpu.SemaphoreType.DMA((61,)),
+        line=[
+            line_landing(tall, LATE_TILES * 128, False), line_landing(tall, d - LATE_TILES * 128, True),
+            line_landing(short, ff // 2, True), line_landing(short, ff // 2, True),
+        ],
+        send_sem=pltpu.SemaphoreType.DMA((2,)), recv_sem=pltpu.SemaphoreType.DMA((91,)),
         mine_sem=pltpu.SemaphoreType.DMA((5,)), tile_sem=pltpu.SemaphoreType.DMA((2,)),
-    )
-    names = {**dict(lengths=lengths), **inputs, **in_hbm, **in_vmem, **scratch}
+        load_sem=pltpu.SemaphoreType.DMA((6,)), store_sem=pltpu.SemaphoreType.DMA((7,)),
+    )
+    names = {**dict(lengths=lengths), **near, **distant, **results, **scratch}
     found = pl.pallas_call(
         functools.partial(step_kernel, shape_of(names)),
-        out_shape=[*leaves(in_hbm), *leaves(in_vmem)],
+        out_shape=leaves(results),
         in_specs=[pl.BlockSpec(memory_space=pltpu.SMEM)]
-        + [pl.BlockSpec(memory_space=v)] * len(leaves(inputs)),
-        out_specs=[pl.BlockSpec(memory_space=pltpu.HBM)] * len(leaves(in_hbm))
-        + [pl.BlockSpec(memory_space=v)] * len(leaves(in_vmem)),
+        + [pl.BlockSpec(memory_space=v)] * len(leaves(near))
+        + [pl.BlockSpec(memory_space=pltpu.HBM)] * len(leaves(distant)),
+        out_specs=[pl.BlockSpec(memory_space=pltpu.HBM)] * len(leaves(results)),
         scratch_shapes=leaves(scratch),
         compiler_params=pltpu.CompilerParams(
             collective_id=1, has_side_effects=True, vmem_limit_bytes=67_000_000
         ),
         name="fused_step",
-    )(lengths, *leaves(inputs))
-    return Box(unpack(shape_of({**in_hbm, **in_vmem}), iter(found)))
+    )(lengths, *leaves(near), *leaves(distant))
+    return Box(unpack(shape_of(results), iter(found)))
 
 
 def adam_kernel(shape, *refs):

time: 247 us -> 227 us (0.919)
  Pallas kernels: 246 us -> 225 us
    pallas_call x1, Pallas kernels: 239 us -> 218 us  [fused_step(): pl.pallas_call(functools.partial(step_kernel, shape_of(names)), out_shape...]
where the time goes in v4:
time: 227 us; the launch traced here: 226 us
  Pallas kernels  225 us (99%)
    pallas_call x1, Pallas kernels, fused_step(): pl.pallas_call(functools.partial(step_kernel, shape_of(names)), out_shape...  218 us
    pallas_call x1, Pallas kernels, adam(): pl.pallas_call(functools.partial(adam_kernel, shape), grid=(steps,), out_...  7.44 us

profile of v4, /device:TPU:0, one launch (start us, length us, event | category | flops | bytes accessed | tf_op | source)
XLA Modules:
  0.0 226.0 jit_solution(3635977488509746069)
XLA Ops:
  0.7 217.9 %fused_step.1 = (bf16[4,2,2,2,16,128]{5,4,3,2,1,0:T(8,128)(2,1)}, bf16[4,2,2,2,32,1024]{5,4,3,2,1,0:T(8,128)(2,1)}, bf16[4,2,2,2,32,3072]{5,4,3,2,1,0:T(8,128)(2...) custom-call(s32[2]{0:T(128)} %refs_0_.2, ...), custom_call_target="tpu_custom_call" | custom-call | tf_op jit(solution)/shard_map/fused_step/pallas_call | solution.py:1400
  218.6 7.4 %adam.1 = (f32[8,32]{1,0:T(8,128)}, f32[1,128]{1,0:T(1,128)}, f32[32,3072]{1,0:T(8,128)}, f32[32,1024]{1,0:T(8,128)}, f32[32,4096]{1,0:T(8,128)}, /*index=5*/f32...) custom-call(f32[8,32]{1,0:T(8,128)} %refs_0_.3, ...), custom_call_target="tpu_custom_call" | custom-call | tf_op jit(solution)/shard_map/adam/pallas_call | solution.py:1480

commit v5 on v4

--- a/solution.py
+++ b/solution.py
@@ -815,9 +815,9 @@
 GATHER_ORDERS = ((0, 1, 2), (0, 2, 1), (2, 1, 0))
 REDUCE_ORDERS = ((2, 1, 0), (1, 2, 0), (0, 1, 2))
 SIZES = (4, 2, 2)
-EARLY_TILES = 4
+EARLY_TILES = 2
+EARLY_UP = 8
 LATE_TILES = 4
-UP_EIGHTHS = (0, 0)
 TILE = 512
 
 
@@ -871,18 +871,21 @@
         mine.append(copy)
     short, tall = r.low[OUT].shape[0], r.low[DOWN].shape[0]
     all_short = (0, short)
-    half, half_ff, early = 3 * d // 2, ff // 2, EARLY_TILES * 128
+    half, early, early_up = 3 * d // 2, EARLY_TILES * 128, EARLY_UP * 128
+    mid_ff, end_ff = (ff - early_up) // 2, ff - early_up
     rest = in_thirds(d - early, 0)
     first = Chunk(wires, [part(SMALL, (0, 16), 0, (1,), False), part(OUT, all_short, 0, in_thirds(d, 0), False)])
     qkv0 = Chunk(wires, [part(QKV, all_short, 0, in_thirds(half, 0), True)])
     qkv1 = Chunk(wires, [part(QKV, all_short, half, in_thirds(half, 0), True)])
-    up0 = Chunk(wires, [part(UP, all_short, 0, in_thirds(half_ff, UP_EIGHTHS[0]), True)])
-    up1 = Chunk(wires, [part(UP, all_short, half_ff, in_thirds(half_ff, UP_EIGHTHS[1]), True)])
+    up0 = Chunk(wires, [part(UP, all_short, 0, in_thirds(mid_ff, 0), True)])
+    up1 = Chunk(wires, [part(UP, all_short, mid_ff, in_thirds(mid_ff, 0), True)])
+    ahead_up = Chunk(wires, [part(UP, all_short, end_ff, (EARLY_UP,), True, GATHER_ORDERS[2:])])
     ahead = Chunk(wires, [part(DOWN, (0, tall), d - early, (EARLY_TILES,), True, GATHER_ORDERS[2:])])
     down0 = Chunk(wires, [part(DOWN, (0, tall // 2), 0, rest, True)])
     down1 = Chunk(wires, [part(DOWN, (tall // 2, tall // 2), 0, rest, True)])
 
     first.start(0)
+    ahead_up.start(0)
     ahead.start(0)
     qkv0.start(0)
     qkv1.start(0)
@@ -901,7 +904,7 @@
     chunks(rows, 32, norm_one)
     for copy in mine:
         copy.wait()
-    ahead.land(0)
+    ahead_up.land(0)
     first.land(0)
     qkv0.land(0)
     up0.start(0)
@@ -911,18 +914,20 @@
     up0.land(0)
     qkv0.land(1)
     up1.start(0)
+    ahead.land(0)
     qkv1.relay(1)
     first.land(2)
     qkv1.land(1)
     up0.relay(1)
     qkv0.land(2)
-    ahead.land(1)
+    ahead_up.land(1)
     up1.land(0)
     up0.land(1)
     down0.start(0)
     up1.relay(1)
     qkv1.land(2)
     first.finish()
+    ahead_up.land(2)
     qkv0.land(3)
     copy = pltpu.make_async_copy(r.full[SMALL], r.smalls, r.mine_sem.at[0])
     copy.start()
@@ -945,7 +950,8 @@
     up1.land(1)
     up0.land(2)
     down1.start(0)
-    ahead.land(2)
+    ahead.land(1)
+    ahead_up.relay(3)
     down0.relay(1)
     qkv1.land(3)
     qkv0.finish()
@@ -1019,10 +1025,11 @@
 
     down1.relay(1)
     up0.land(3)
+    ahead.land(2)
+    ahead_up.land(3)
     lax.fori_loop(0, heads2 // 2, attend, 0)
     down1.land(1)
     down0.land(2)
-    ahead.relay(3)
     lax.fori_loop(heads2 // 2, heads2, attend, 0)
     attn_far = transpose_out(r.attn, r.attn_t, r.attn_far)
 
@@ -1031,8 +1038,7 @@
         r.h1[:, span] = r.tokens[:, span].astype(F32) + nn(r.attn[...], tile) + vec[4:5, span]
 
     tile_stream(OUT, 0, d, out_tile)
-    up1.land(3)
-    up0.finish()
+    ahead.relay(3)
 
     def second_in(span):
         normed, _ = row_stats(r.h1[span, :])
@@ -1040,7 +1046,6 @@
 
     chunks(rows, 32, second_in)
     two_far = transpose_out(r.a, r.two_t, r.two_far)
-    down1.land(2)
 
     def up_tile(i, tile):
         pre = nn(r.a[...], tile) + bias[:, columns_of(i, TILE)]
@@ -1048,13 +1053,20 @@
         r.act[:, columns_of(i, TILE)] = value.astype(BF16)
         r.slope[:, columns_of(i, TILE)] = slope.astype(BF16)
 
-    tile_stream(UP, 0, ff // 2, up_tile)
-    act_far0 = transpose_out(r.act, r.act_t, r.act_far, 0, 8)
+    ahead_up.finish()
+    tile_stream(UP, end_ff, ff, up_tile)
+    up0.finish()
+    down1.land(2)
+    up1.land(3)
+    tile_stream(UP, 0, mid_ff, up_tile)
+    act_far0 = transpose_out(r.act, r.act_t, r.act_far, 0, mid_ff // 256)
+    act_far2 = transpose_out(r.act, r.act_t, r.act_far, end_ff // 256, 16)
+    up1.finish()
+    tile_stream(UP, mid_ff, end_ff, up_tile)
+    act_far1 = transpose_out(r.act, r.act_t, r.act_far, mid_ff // 256, end_ff // 256)
     down0.land(3)
-    up1.finish()
-    tile_stream(UP, ff // 2, ff, up_tile)
-    act_far1 = transpose_out(r.act, r.act_t, r.act_far, 8, 16)
     dy_swap.wait()
+    act_far2.wait()
     act_far0.wait()
     act_far1.wait()
 
@@ -1299,7 +1311,6 @@
     advance(5, 1)
     reduces[7].start(0)
     up_lines[1].across()
-    line.second()
     down_line.complete(r.fin[DOWN])
     advance(6, 1)
     up_lines[0].back()
@@ -1307,13 +1318,12 @@
     advance(5, 2)
     up_lines[1].back()
     advance(7, 1)
+    line.second()
     advance(6, 2)
-    line.third()
     up_lines[0].complete(r.fin[UP])
     advance(7, 2)
     advance(8, 1)
-    line.finish(r.fin[DOWN])
-    keep(r.fin[DOWN], r.final[DOWN])
+    line.third()
     advance(8, 2)
     up_lines[1].complete(r.fin[UP])
     complete(4, OUT)
@@ -1321,6 +1331,8 @@
     complete(5, QKV)
     keep(r.fin[OUT], r.final[OUT])
     complete(6, QKV)
+    line.finish(r.fin[DOWN])
+    keep(r.fin[DOWN], r.final[DOWN])
     complete(8, SMALL)
     keep(r.fin[SMALL], r.final[SMALL])
     complete(7, QKV)
@@ -1392,7 +1404,7 @@
             line_landing(tall, LATE_TILES * 128, False), line_landing(tall, d - LATE_TILES * 128, True),
             line_landing(short, ff // 2, True), line_landing(short, ff // 2, True),
         ],
-        send_sem=pltpu.SemaphoreType.DMA((2,)), recv_sem=pltpu.SemaphoreType.DMA((91,)),
+        send_sem=pltpu.SemaphoreType.DMA((2,)), recv_sem=pltpu.SemaphoreType.DMA((97,)),
         mine_sem=pltpu.SemaphoreType.DMA((5,)), tile_sem=pltpu.SemaphoreType.DMA((2,)),
         load_sem=pltpu.SemaphoreType.DMA((6,)), store_sem=pltpu.SemaphoreType.DMA((7,)),
     )

time: 227 us -> 217 us (0.956)
  Pallas kernels: 225 us -> 215 us
    pallas_call x1, Pallas kernels: 218 us -> 208 us  [fused_step(): pl.pallas_call(functools.partial(step_kernel, shape_of(names)), out_shape...]
where the time goes in v5:
time: 217 us; the launch traced here: 216 us
  Pallas kernels  215 us (99%)
    pallas_call x1, Pallas kernels, fused_step(): pl.pallas_call(functools.partial(step_kernel, shape_of(names)), out_shape...  208 us
    pallas_call x1, Pallas kernels, adam(): pl.pallas_call(functools.partial(adam_kernel, shape), grid=(steps,), out_...  7.44 us

profile of v5, /device:TPU:0, one launch (start us, length us, event | category | flops | bytes accessed | tf_op | source)
XLA Modules:
  0.0 215.7 jit_solution(14793037870252929456)
XLA Ops:
  0.7 207.6 %fused_step.1 = (bf16[4,2,2,2,16,128]{5,4,3,2,1,0:T(8,128)(2,1)}, bf16[4,2,2,2,32,1024]{5,4,3,2,1,0:T(8,128)(2,1)}, bf16[4,2,2,2,32,3072]{5,4,3,2,1,0:T(8,128)(2...) custom-call(s32[2]{0:T(128)} %refs_0_.2, ...), custom_call_target="tpu_custom_call" | custom-call | tf_op jit(solution)/shard_map/fused_step/pallas_call | solution.py:1412
  208.3 7.4 %adam.1 = (f32[8,32]{1,0:T(8,128)}, f32[1,128]{1,0:T(1,128)}, f32[32,3072]{1,0:T(8,128)}, f32[32,1024]{1,0:T(8,128)}, f32[32,4096]{1,0:T(8,128)}, /*index=5*/f32...) custom-call(f32[8,32]{1,0:T(8,128)} %refs_0_.3, ...), custom_call_target="tpu_custom_call" | custom-call | tf_op jit(solution)/shard_map/adam/pallas_call | solution.py:1492

commit v6 on v5

--- a/solution.py
+++ b/solution.py
@@ -854,9 +854,12 @@
         block[0:8, k * narrow:(k + 1) * narrow] = r.vectors[...] * here
     block[8:9, :] = r.bias_up[...]
     r.low[SMALL][...] = block[...].astype(BF16)
-    for at, which in enumerate((OUT, QKV, UP, DOWN)):
+
+    def lower(at, which):
         loads[at].wait()
         r.low[which][...] = r.fin[which][...].astype(BF16)
+
+    lower(0, OUT)
     pl.semaphore_wait(barrier, len(others))
     wires = Wires(r.send_sem, r.recv_sem, r.gauge, partner)
 
@@ -864,11 +867,6 @@
         colours = split_colours(start, shares, orders)
         return Spread(r.full[which], r.low[which], row_range, colours, relay, place)
 
-    mine = []
-    for which in (SMALL, OUT, QKV, UP, DOWN):
-        copy = pltpu.make_async_copy(r.low[which], r.full[which].at[(*coords, core)], r.mine_sem.at[which])
-        copy.start()
-        mine.append(copy)
     short, tall = r.low[OUT].shape[0], r.low[DOWN].shape[0]
     all_short = (0, short)
     half, early, early_up = 3 * d // 2, EARLY_TILES * 128, EARLY_UP * 128
@@ -885,10 +883,18 @@
     down1 = Chunk(wires, [part(DOWN, (tall // 2, tall // 2), 0, rest, True)])
 
     first.start(0)
+    lower(2, UP)
     ahead_up.start(0)
-    ahead.start(0)
+    lower(1, QKV)
     qkv0.start(0)
     qkv1.start(0)
+    lower(3, DOWN)
+    ahead.start(0)
+    mine = []
+    for which in (SMALL, OUT, QKV, UP, DOWN):
+        copy = pltpu.make_async_copy(r.low[which], r.full[which].at[(*coords, core)], r.mine_sem.at[which])
+        copy.start()
+        mine.append(copy)
     loads[4].wait()
     for slot in range(slots):
         span = pl.ds(slot * MB_ROWS, MB_ROWS)
@@ -1454,7 +1460,7 @@
 
 
 def adam(found, params, moments):
-    steps = 4
+    steps = 2
 
     def whole(s):
         return pl.BlockSpec(s, lambda i: (0,) * len(s))

time: 217 us -> 215 us (level)
  no operation moved by 1% of the time
where the time goes in v6:
time: 215 us
  Pallas kernels  214 us (100%)
    pallas_call x1, Pallas kernels, fused_step(): pl.pallas_call(functools.partial(step_kernel, shape_of(names)), out_shape...  208 us
    pallas_call x1, Pallas kernels, adam(): pl.pallas_call(functools.partial(adam_kernel, shape), grid=(steps,), out_...  6.25 us

profile of v6, /device:TPU:0, one launch (start us, length us, event | category | flops | bytes accessed | tf_op | source)
XLA Modules:
  0.0 214.5 jit_solution(15277033615345723799)
XLA Ops:
  0.7 207.6 %fused_step.1 = (bf16[4,2,2,2,16,128]{5,4,3,2,1,0:T(8,128)(2,1)}, bf16[4,2,2,2,32,1024]{5,4,3,2,1,0:T(8,128)(2,1)}, bf16[4,2,2,2,32,3072]{5,4,3,2,1,0:T(8,128)(2...) custom-call(s32[2]{0:T(128)} %refs_0_.2, ...), custom_call_target="tpu_custom_call" | custom-call | tf_op jit(solution)/shard_map/fused_step/pallas_call | solution.py:1418
  208.3 6.3 %adam.1 = (f32[8,32]{1,0:T(8,128)}, f32[1,128]{1,0:T(1,128)}, f32[32,3072]{1,0:T(8,128)}, f32[32,1024]{1,0:T(8,128)}, f32[32,4096]{1,0:T(8,128)}, /*index=5*/f32...) custom-call(f32[8,32]{1,0:T(8,128)} %refs_0_.3, ...), custom_call_target="tpu_custom_call" | custom-call | tf_op jit(solution)/shard_map/adam/pallas_call | solution.py:1498

commit v7 on v6

--- a/solution.py
+++ b/solution.py
@@ -1460,7 +1460,7 @@
 
 
 def adam(found, params, moments):
-    steps = 2
+    steps = 1
 
     def whole(s):
         return pl.BlockSpec(s, lambda i: (0,) * len(s))

time: 215 us -> 216 us (level)
  no operation moved by 1% of the time
where the time goes in v7:
time: 216 us; the launch traced here: 215 us
  Pallas kernels  215 us (100%)
    pallas_call x1, Pallas kernels, fused_step(): pl.pallas_call(functools.partial(step_kernel, shape_of(names)), out_shape...  208 us
    pallas_call x1, Pallas kernels, adam(): pl.pallas_call(functools.partial(adam_kernel, shape), grid=(steps,), out_...  7.05 us

profile of v7, /device:TPU:0, one launch (start us, length us, event | category | flops | bytes accessed | tf_op | source)
XLA Modules:
  0.0 215.5 jit_solution(7463618590272928358)
XLA Ops:
  0.7 207.6 %fused_step.1 = (bf16[4,2,2,2,16,128]{5,4,3,2,1,0:T(8,128)(2,1)}, bf16[4,2,2,2,32,1024]{5,4,3,2,1,0:T(8,128)(2,1)}, bf16[4,2,2,2,32,3072]{5,4,3,2,1,0:T(8,128)(2...) custom-call(s32[2]{0:T(128)} %refs_0_.2, ...), custom_call_target="tpu_custom_call" | custom-call | tf_op jit(solution)/shard_map/fused_step/pallas_call | solution.py:1418
  208.3 7.1 %adam.1 = (f32[8,32]{1,0:T(8,128)}, f32[1,128]{1,0:T(1,128)}, f32[32,3072]{1,0:T(8,128)}, f32[32,1024]{1,0:T(8,128)}, f32[32,4096]{1,0:T(8,128)}, /*index=5*/f32...) custom-call(f32[8,32]{1,0:T(8,128)} %refs_0_.3, ...), custom_call_target="tpu_custom_call" | custom-call | tf_op jit(solution)/shard_map/adam/pallas_call | solution.py:1498
